TPU v7x, 256 devices: a whole 4x4x8 slice. The times are simulated.
256 devices in a mesh: seq: 16 (over z_lo, x), tp: 8 (over y, core), grp: 2 (over z_hi).
Axes of the slice: x: 4, y: 4, z: 8 (z_hi: 2, z_lo: 4; z = z_hi * 4 + z_lo), core: 2. Of those that a mesh axis runs over, the one named last changes fastest.
Arguments:
- prefill_query: bfloat16 [2, 6144, 8192], P('grp', 'seq', 'tp'), may hold values from -6 to 6
- prefill_keys: bfloat16 [2, 6144, 1024], P('grp', 'seq', 'tp'), may hold values from -6 to 6
- prefill_values: bfloat16 [2, 6144, 1024], P('grp', 'seq', 'tp'), may hold values from -6 to 6
- decode_query: bfloat16 [2, 128, 4, 8192], P('grp', 'seq', None, 'tp'), may hold values from -6 to 6
- decode_keys: bfloat16 [2, 128, 4, 1024], P('grp', 'seq', None, 'tp'), may hold values from -6 to 6
- decode_values: bfloat16 [2, 128, 4, 1024], P('grp', 'seq', None, 'tp'), may hold values from -6 to 6
- page_table: int32 [2, 128, 16], P('grp', 'seq'), may hold values from 0 to 47
- context_lengths: int32 [2, 128], P('grp', 'seq'), may hold values from 1 to 2048
- check_rows: bfloat16 [8, 128], replicated, may hold values from -0.125 to 0.125
Outputs:
- prefill_out: bfloat16 [2, 6144, 8192], P('grp', 'seq', 'tp')
- decode_out: bfloat16 [2, 128, 4, 8192], P('grp', 'seq', None, 'tp')
- page_digest: float32 [2, 128, 8, 2048], P('grp', 'seq', None, 'tp')
Inputs may be any that keep to these rules, and one draw needn't show every extreme that they name: page_table[g, r, j] names the page of 128 tokens of prompt 1 - g that holds context tokens j * 128 to j * 128 + 127 of request r; pages may repeat. Request r reads its first context_lengths[g, r] context tokens.
All inputs are finite; a program needn't handle non-finite values.
Results may differ from a plain program's by a relative error of at most 0.014.
Values may be sent and summed in bfloat16 or wider, within the bound.
No kernel may reach another device: no remote copies, remote signals or barrier semaphores. Data moves between devices by JAX's collectives and lax.ppermute only.
A program may use at most 64 MiB of HBM per device.

v0:
```python
import math

import jax
import jax.numpy as jnp
from jax import lax
from jax.sharding import Mesh
from jax.sharding import PartitionSpec as P

HQ = 64
KVH = 8
HD = 128
PAGE = 128
SEQ = ("seq_0", "seq_1")


neg_large = -1e30


def in_order(parts, dim):
    shape = list(parts.shape[1:])
    shape[dim] *= parts.shape[0]
    return jnp.moveaxis(parts, 0, dim).reshape(shape)


def gather_in_order(shard, axes, turns):
    parts = shard[None]
    for k in turns:
        parts = lax.all_gather(parts, axes[k], axis=0, tiled=True)
    held = [lax.axis_size(axes[k]) for k in reversed(turns)]
    parts = parts.reshape(*held, *shard.shape)
    turned = sorted(range(len(turns)), key=lambda place: turns[len(turns) - 1 - place])
    return parts.transpose(*turned, *range(len(turns), parts.ndim)).reshape(-1, *shard.shape)


def gathered_by_axis(shard, axes, turns, dim):
    return in_order(gather_in_order(shard, axes, turns), dim)


def partner(shard, axis, apart):
    return lax.ppermute(shard, axis, [(i, i ^ 1 << apart) for i in range(lax.axis_size(axis))])


def from_everyone(shard, axis):
    peers = lax.axis_size(axis)
    return lax.all_to_all(
        jnp.broadcast_to(shard[None], (peers, *shard.shape)), axis, 0, 0, tiled=True
    )


def gathered_copies(shard, axis, dim):
    return in_order(from_everyone(shard, axis), dim)


def side_by_side(arrays, axis, split_dim, concat_dim, along):
    widths = [math.prod(a.shape[along:]) for a in arrays]
    both = jnp.concatenate(
        [a.reshape(*a.shape[:along], w) for a, w in zip(arrays, widths)], axis=along
    )
    out = lax.all_to_all(both, axis, split_axis=split_dim, concat_axis=concat_dim, tiled=True)
    parts = jnp.split(out, [sum(widths[:k]) for k in range(1, len(widths))], axis=along)
    return tuple((b.reshape(*out.shape[:along], *a.shape[along:]) for a, b in zip(arrays, parts)))


def for_sending(shard):
    return jax.tree.map(lambda a: a.astype(jnp.bfloat16) if a.dtype == jnp.float32 else a, shard)


def fold_block(folded, query_heads, key_block, value_block, columns, places):
    running_max, totals, summed = folded
    col_count = key_block.shape[0]
    kv_local = query_heads.shape[1]
    key_heads = key_block.reshape(col_count, kv_local, HD)
    value_heads = value_block.reshape(col_count, kv_local, HD)
    scores = jnp.einsum(
        "rkgd,ckd->kgrc", query_heads, key_heads, preferred_element_type=jnp.float32
    ) * (1.0 / math.sqrt(HD))
    allowed = columns[None, :] <= places[:, None]
    scores = jnp.where(allowed, scores, neg_large)
    new_max = jnp.maximum(running_max, jnp.max(scores, axis=-1))
    weights = jnp.where(allowed, jnp.exp(scores - new_max[..., None]), 0.0)
    fading = jnp.exp(running_max - new_max)
    totals = totals * fading + jnp.sum(weights, axis=-1)
    update = jnp.einsum(
        "kgrc,ckd->rkgd",
        weights.astype(jnp.bfloat16),
        value_heads,
        preferred_element_type=jnp.float32,
    )
    summed = summed * jnp.transpose(fading, (2, 0, 1))[..., None] + update
    return (new_max, totals, summed)


def attend_piece(folded, query_heads, key_rows, value_rows, columns, places):
    piece_rows = key_rows.shape[0]
    block_rows = math.gcd(1024, piece_rows)
    block_count = piece_rows // block_rows
    key_blocks = key_rows.reshape(block_count, block_rows, key_rows.shape[1])
    value_blocks = value_rows.reshape(block_count, block_rows, value_rows.shape[1])
    column_blocks = columns.reshape(block_count, block_rows)

    def advance(partial_state, member):
        key_block, value_block, column_block = member
        return (
            fold_block(partial_state, query_heads, key_block, value_block, column_block, places),
            None,
        )

    folded, ignored = lax.scan(advance, folded, (key_blocks, value_blocks, column_blocks))
    return folded


def split_halves(product):
    upper = product.astype(jnp.bfloat16)
    lower = (product - upper.astype(jnp.float32)).astype(jnp.bfloat16)
    return (upper, lower)


def remote_context(all_query, all_table, all_lengths, key_rows, value_rows, check_rows, first_page):
    asked_count, max_pages = all_table.shape
    row_count = key_rows.shape[0]
    kv_local = key_rows.shape[1] // HD
    own_pages = row_count // PAGE
    offsets = jnp.arange(PAGE, dtype=jnp.int32)
    page_hits = (
        all_table[:, :, None] == first_page + jnp.arange(own_pages, dtype=jnp.int32)[None, None, :]
    ).astype(jnp.float32)
    token_place = jnp.arange(max_pages, dtype=jnp.int32)[:, None] * PAGE + offsets[None, :]
    token_fits = (token_place[None] < all_lengths[:, None, None]).astype(jnp.float32)
    counts = jnp.einsum("ajp,ajo->apo", page_hits, token_fits).reshape(asked_count, row_count)
    key_heads = key_rows.reshape(row_count, kv_local, HD)
    value_heads = value_rows.reshape(row_count, kv_local, HD)
    scores = jnp.einsum(
        "askgd,ckd->askgc", all_query, key_heads, preferred_element_type=jnp.float32
    ) * (1.0 / math.sqrt(HD))
    live_mask = (counts > 0)[:, None, None, None, :]
    scores = jnp.where(live_mask, scores, neg_large)
    highest = jnp.max(scores, axis=-1)
    weights = jnp.where(live_mask, jnp.exp(scores - highest[..., None]), 0.0)
    repeats = counts[:, None, None, None, :]
    totals = jnp.sum(weights * repeats, axis=-1)
    weighted = lax.optimization_barrier(weights.astype(jnp.bfloat16)).astype(jnp.float32) * repeats
    weight_upper, weight_lower = split_halves(weighted)
    summed = jnp.einsum(
        "askgc,ckd->askgd", weight_upper, value_heads, preferred_element_type=jnp.float32
    )
    summed = summed + jnp.einsum(
        "askgc,ckd->askgd", weight_lower, value_heads, preferred_element_type=jnp.float32
    )
    paired = jnp.concatenate(
        [key_rows.reshape(row_count, kv_local, HD), value_rows.reshape(row_count, kv_local, HD)],
        axis=-1,
    )
    paired = paired.reshape(own_pages, PAGE, kv_local, 2 * HD)
    counted_checks = (
        counts.reshape(asked_count, own_pages, 1, PAGE) * check_rows.astype(jnp.float32)[None, None]
    )
    check_upper, check_lower = split_halves(counted_checks)
    digest = jnp.einsum("apco,poke->acke", check_upper, paired, preferred_element_type=jnp.float32)
    digest = digest + jnp.einsum(
        "apco,poke->acke", check_lower, paired, preferred_element_type=jnp.float32
    )
    return (highest, totals, summed, digest)


def finish(highest, totals, summed, asking, new_keys, new_values):
    requests, step_count, kv_local = (asking.shape[0], asking.shape[1], asking.shape[2])
    key_heads = new_keys.reshape(requests, step_count, kv_local, HD)
    value_heads = new_values.reshape(requests, step_count, kv_local, HD)
    fresh_scores = jnp.einsum(
        "rskgd,rjkd->rskgj", asking, key_heads, preferred_element_type=jnp.float32
    ) * (1.0 / math.sqrt(HD))
    step_order = jnp.arange(step_count, dtype=jnp.int32)
    causal = (step_order[None, :] <= step_order[:, None])[None, :, None, None, :]
    fresh_scores = jnp.where(causal, fresh_scores, neg_large)
    joint_max = jnp.maximum(highest, jnp.max(fresh_scores, axis=-1))
    fresh_weights = jnp.where(causal, jnp.exp(fresh_scores - joint_max[..., None]), 0.0)
    fading = jnp.exp(highest - joint_max)
    totals = totals * fading + jnp.sum(fresh_weights, axis=-1)
    summed = summed * fading[..., None] + jnp.einsum(
        "rskgj,rjkd->rskgd",
        fresh_weights.astype(jnp.bfloat16),
        value_heads,
        preferred_element_type=jnp.float32,
    )
    return (summed / totals[..., None]).reshape(requests, step_count, -1).astype(jnp.bfloat16)


def shards(
    prefill_query,
    prefill_keys,
    prefill_values,
    decode_query,
    decode_keys,
    decode_values,
    page_table,
    context_lengths,
    check_rows,
):
    groups = HQ // KVH
    key_rows = prefill_keys[0]
    value_rows = prefill_values[0]
    row_count = key_rows.shape[0]
    kv_local = key_rows.shape[1] // HD
    members = lax.axis_size(SEQ)
    own_index = lax.axis_index(SEQ)
    held_query = prefill_query[0]
    query_heads = held_query.reshape(row_count, kv_local, groups, HD)
    places = own_index * row_count + jnp.arange(row_count, dtype=jnp.int32)
    start_state = (
        jnp.full((kv_local, groups, row_count), neg_large, jnp.float32),
        jnp.zeros((kv_local, groups, row_count), jnp.float32),
        jnp.zeros((row_count, kv_local, groups, HD), jnp.float32),
    )
    shard_pair = (
        gathered_by_axis(key_rows, SEQ, (0, 1), 0),
        gathered_by_axis(value_rows, SEQ, (0, 1), 0),
    )
    piece_rows = shard_pair[0].shape[0]
    columns = jnp.arange(piece_rows, dtype=jnp.int32)
    running_max, totals, summed = attend_piece(
        start_state, query_heads, shard_pair[0], shard_pair[1], columns, places
    )
    held_out = (
        (summed / jnp.transpose(totals, (2, 0, 1))[..., None])
        .reshape(row_count, -1)
        .astype(jnp.bfloat16)
    )
    prefill_out = held_out[None]
    requests = decode_query.shape[1]
    step_count = decode_query.shape[2]
    asking = decode_query[0].reshape(requests, step_count, kv_local, groups, HD)
    own_table = page_table[0]
    lengths = context_lengths[0]
    sent_query, sent_table, sent_lengths = partner((decode_query[0], own_table, lengths), "grp", 0)
    all_query, all_table, all_lengths = (
        gathered_copies(sent_query, SEQ, 0),
        gathered_copies(sent_table, SEQ, 0),
        gathered_copies(sent_lengths, SEQ, 0),
    )
    asked_count = all_query.shape[0]
    partials = remote_context(
        all_query.reshape(asked_count, step_count, kv_local, groups, HD),
        all_table,
        all_lengths,
        key_rows,
        value_rows,
        check_rows,
        own_index * (row_count // PAGE),
    )
    by_owner = [member.reshape((members, requests) + member.shape[1:]) for member in partials]
    got_max, got_totals, got_summed, got_digest = tuple(
        (
            part.astype(jnp.float32)
            for part in side_by_side(
                (
                    by_owner[0].astype(jnp.bfloat16),
                    by_owner[1].astype(jnp.bfloat16),
                    by_owner[2].astype(jnp.bfloat16),
                    by_owner[3].astype(jnp.bfloat16),
                ),
                SEQ,
                0,
                0,
                2,
            )
        )
    )
    overall = jnp.max(got_max, axis=0)
    fading = jnp.exp(got_max - overall[None])
    merged_totals = jnp.sum(got_totals * fading, axis=0)
    merged_summed = jnp.sum(got_summed * fading[..., None], axis=0)
    merged_digest = jnp.sum(got_digest, axis=0)
    highest, ctx_totals, ctx_summed, digest = (
        partner(for_sending(overall), "grp", 0).astype(overall.dtype),
        partner(for_sending(merged_totals), "grp", 0).astype(merged_totals.dtype),
        partner(for_sending(merged_summed), "grp", 0).astype(merged_summed.dtype),
        partner(for_sending(merged_digest), "grp", 0).astype(merged_digest.dtype),
    )
    decode_out = finish(highest, ctx_totals, ctx_summed, asking, decode_keys[0], decode_values[0])[
        None
    ]
    page_digest = digest.reshape(requests, digest.shape[1], -1)[None]
    return (prefill_out, decode_out, page_digest)


def solution(mesh):
    split = Mesh(
        mesh.devices.reshape(4, 4, mesh.shape["tp"], mesh.shape["grp"]),
        ("seq_0", "seq_1", "tp", "grp"),
    )
    placed = (
        P("grp", SEQ, "tp"),
        P("grp", SEQ, "tp"),
        P("grp", SEQ, "tp"),
        P("grp", SEQ, None, "tp"),
        P("grp", SEQ, None, "tp"),
        P("grp", SEQ, None, "tp"),
        P("grp", SEQ, None),
        P("grp", SEQ),
        P(),
    )
    return jax.shard_map(
        shards,
        mesh=split,
        in_specs=placed,
        out_specs=(P("grp", SEQ, "tp"), P("grp", SEQ, None, "tp"), P("grp", SEQ, None, "tp")),
        check_vma=False,
    )
```

profile of v0, /device:TPU:10, one launch (start us, length us, event | category | flops | bytes accessed | tf_op | source)
XLA Modules:
  0.0 306.1 jit_solution(18319489041053806043)
XLA Ops:
  7.3 17.8 %all_gather.12 = bf16[4,384,128]{2,1,0:T(8,128)(2,1)} all-gather(bf16[1,384,128]{2,1,0:T(8,128)(2,1)} %param.12), channel_id=1, replica_groups=mesh['seq_0'=4,'seq_1'=4,'tp'=8,'grp'=2] {'seq_0'}, dimensions={0}, use_global_device_ids=true | all-gather | bytes 491520 | tf_op jit(solution)/shard_map/all_gather | solution.py:28
  25.1 4.9 %collective-permute-start.2 = (bf16[8,4,1024]{2,1,0:T(4,128)(2,1)}, bf16[8,4,1024]{2,1,0:T(4,128)(2,1)S(1)}, u32[]{:S(2)}, u32[]{:S(2)}) collective-permute-start(bf16[8,4,1024]{2,1,0:T(4,128)(2,1)} %bitcast.277), channel_id=1, source_target_pairs={{0,1},{1,0},{2,3},{3,2},{4,5},{5,4},{6,7},{7,6},{8,9},{9,8},{10,11... | collective-permute-start | bytes 196616 | tf_op jit(solution)/shard_map/ppermute | solution.py:40
  30.0 1.1 collective-permute-start.1
  31.1 6.5 %collective-permute-done.1 = s32[8]{0:T(128)S(1)} collective-permute-done((s32[8]{0:T(128)}, s32[8]{0:T(128)S(1)}, u32[]{:S(2)}, u32[]{:S(2)}) %collective-permute-start.1) | collective-permute-done | bytes 64 | tf_op jit(solution)/shard_map/ppermute | solution.py:40
  38.2 6.3 %all-to-all-start.1 = ((s32[16,1,8]{2,1,0:T(1,128)}), s32[16,1,8]{2,1,0:T(1,128)S(1)}, u32[]{:S(2)}, u32[]{:S(2)}) async-start(s32[16,1,8]{2,1,0:T(1,128)} %broadcast_in_dim.103), calls=%async_computation.1 | async-start | bytes 16384 | tf_op jit(solution)/shard_map/all_to_all | solution.py:45
  44.5 1.5 collective-permute-start
  46.1 6.2 %collective-permute-done = s32[8,16]{1,0:T(8,128)S(1)} collective-permute-done((s32[8,16]{1,0:T(8,128)}, s32[8,16]{1,0:T(8,128)S(1)}, u32[]{:S(2)}, u32[]{:S(2)}) %collective-permute-start) | collective-permute-done | bytes 544 | tf_op jit(solution)/shard_map/ppermute | solution.py:40
  52.2 0.7 reshape.374
  52.9 7.5 %all-to-all-start = ((s32[16,1,128]{2,1,0:T(1,128)}), s32[16,1,128]{2,1,0:T(1,128)S(1)}, u32[]{:S(2)}, u32[]{:S(2)}) async-start(s32[16,1,128]{2,1,0:T(1,128)} %reshape.374), calls=%async_computation | async-start | bytes 16384 | tf_op jit(solution)/shard_map/all_to_all | solution.py:45
  60.5 6.5 %all-to-all-done = s32[16,1,128]{2,1,0:T(1,128)S(1)} async-done(((s32[16,1,128]{2,1,0:T(1,128)}), s32[16,1,128]{2,1,0:T(1,128)S(1)}, u32[]{:S(2)}, u32[]{:S(2)}) %all-to-all-start) | async-done | bytes 8224 | tf_op jit(solution)/shard_map/all_to_all | solution.py:45
  67.0 1.1 broadcast_in_dim.105
  68.1 5.0 %all-to-all-start.2 = ((bf16[16,8,4,1024]{3,1,2,0:T(8,128)(2,1)}), bf16[16,8,4,1024]{3,1,2,0:T(8,128)(2,1)S(1)}, u32[]{:S(2)}, u32[]{:S(2)}) async-start(bf16[16,8,4,1024]{3,1,2,0:T(8,128)(2,1)} %broadcast_in_dim.105), calls=%async_computation.2 | async-start | bytes 2097152 | tf_op jit(solution)/shard_map/all_to_all | solution.py:45
  73.2 28.7 %all_gather.14 = bf16[4,384,128]{2,1,0:T(8,128)(2,1)} all-gather(bf16[1,384,128]{2,1,0:T(8,128)(2,1)S(1)} %copy-done.4), channel_id=1, replica_groups=mesh['seq_0'=4,'seq_1'=4,'tp'=8,'grp'=2] {'seq_0'}, dimensions={0}, use_global_device_ids=true | all-gather | bytes 491520 | tf_op jit(solution)/shard_map/all_gather | solution.py:28
  103.5 1.0 fusion.80
  105.1 0.7 reduce.17
  108.8 1.4 fusion.41
  111.2 3.7 %fusion.24 = (f32[128,4,8]{0,2,1:T(8,128)S(1)}, f32[384,128,4,8]{1,0,3,2:T(8,128)}) fusion(pred[128,384]{0,1:T(8,128)(4,1)S(1)} %broadcast_compare_fusion.1, bf16[128,4,8,128]{3,2,0,1:T(8,128)(2,1)S(1)} %bitcast.261, bf16[1,384,128]{2,1,0:T(8,128)(2,1)S(1)} %copy-done.3), kind=kOutput, calls=%fused_computation.36 | convolution fusion | flops 407367680 | bytes 7503872 | tf_op jit(solution)/shard_map/askgd,ckd->askgc/dot_general | solution.py:132
  115.3 5.2 %fusion.25 = (bf16[128,4,1,8,384]{0,4,3,1,2:T(8,128)(2,1)}, bf16[128,4,8]{0,2,1:T(8,128)(2,1)S(1)}) fusion(f32[384,128,4,8]{1,0,3,2:T(8,128)} %get-tuple-element.142, f32[128,4,8]{0,2,1:T(8,128)S(1)} %get-tuple-element.141, pred[128,384]{0,1:T(8,128)(4,1)S(1)} %broadcast_compare_fusion.1, f32[128,384]{0,1:T(8,128)S(1)} %bitcast.258), kind=kLoop, calls=%fused_computation.37 | loop fusion | flops 11005952 | bytes 9707520 | tf_op jit(solution)/shard_map/convert_element_type | solution.py:141
  120.8 3.1 %fusion.27 = f32[128,4,8,128]{3,0,2,1:T(8,128)S(1)} fusion(bf16[128,4,1,8,384]{0,4,3,1,2:T(8,128)(2,1)} %get-tuple-element.135, f32[128,384]{0,1:T(8,128)S(1)} %bitcast.259, bf16[1,384,128]{2,1,0:T(8,128)(2,1)S(1)} %copy-done.5), kind=kOutput, calls=%fused_computation.39 | convolution fusion | flops 407371776 | bytes 5537792 | tf_op jit(solution)/shard_map/askgc,ckd->askgd/dot_general | solution.py:143
  124.0 1.1 fusion.37
  125.1 0.7 copy.72
  126.3 2.7 concatenate.14
  129.0 7.3 %all-to-all-start.3 = ((bf16[16,8,6208]{2,1,0:T(8,128)(2,1)}), bf16[16,8,6208]{2,1,0:T(8,128)(2,1)S(1)}, u32[]{:S(2)}, u32[]{:S(2)}) async-start(bf16[16,8,6208]{2,1,0:T(8,128)(2,1)} %concatenate.14), calls=%async_computation.3 | async-start | bytes 3211264 | tf_op jit(solution)/shard_map/all_to_all | solution.py:59
  136.3 2.7 copy.60
  139.0 2.7 copy.62
  141.8 135.4 %while.15 = (s32[]{:T(128)}, f32[1,8,384]{2,1,0:T(8,128)S(1)}, f32[1,8,384]{2,1,0:T(8,128)S(1)}, f32[384,1,8,128]{0,3,2,1:T(8,128)}, s32[6,1024]{1,0:T(8,128)}, ...) while((s32[]{:T(128)}, f32[1,8,384]{2,1,0:T(8,128)S(1)}, ...), condition=%wide.region_3.4_spmd.clone, body=%wide.region_0.3_spmd.clone.sunk | while | flops 1653098880 | bytes 94321840 | solution.py:108
  141.8 0.8 constant_dynamic-slice_fusion.2
  142.8 7.6 %fusion.89 = (f32[8,384]{1,0:T(8,128)S(1)}, f32[1024,384,8]{1,0,2:T(8,128)}) fusion(pred[384,1024]{0,1:T(8,128)(4,1)S(1)} %broadcast_compare_fusion.3, bf16[384,1,8,128]{3,0,2,1:T(8,128)(2,1)S(1)} %get-tuple-element.236, bf16[6,1024,128]{2,1,0:T(8,128)(2,1)} %get-tuple-element.235, s32[]{:T(128)S(6)} %copy.105), kind=kOutput, calls=%fused_computation.3.clone.1 | convolution fusion | flops 814740480 | bytes 14036996 | tf_op jit(solution)/shard_map/while/body/eval_jaxpr/rkgd,ckd->kgrc/dot_general | solution.py:74
  150.4 6.7 %fusion.91 = f32[8,384]{1,0:T(8,128)S(1)} fusion(f32[1024,384,8]{1,0,2:T(8,128)} %get-tuple-element.206, f32[8,384]{1,0:T(8,128)S(1)} %bitcast.256, pred[384,1024]{0,1:T(8,128)(4,1)S(1)} %broadcast_compare_fusion.3), kind=kLoop, calls=%fused_computation.5.clone.1 | loop fusion | flops 15725568 | bytes 13000704 | tf_op jit(solution)/shard_map/while/body/eval_jaxpr/reduce_sum | solution.py:82
  157.2 1.5 copy-done.1
  158.7 5.4 %bitcast_add_fusion.6 = f32[384,1,8,128]{0,3,2,1:T(8,128)} fusion(f32[384,1,8,128]{0,3,2,1:T(8,128)} %get-tuple-element.222, f32[1024,384,8]{1,0,2:T(8,128)S(1)} %copy-done.1, f32[8,384]{1,0:T(8,128)S(1)} %bitcast.257, pred[384,1024]{0,1:T(8,128)(4,1)S(1)} %broadcast_compare_fusion.3, f32[384,8]{0,1:T(8,128)S(1)} %get-tuple-element.207, ...), kind=kOutput, calls=%fused_computation.9.clone.1 | convolution fusion | flops 822214656 | bytes 16408581 | tf_op jit(solution)/shard_map/while/body/eval_jaxpr/kgrc,ckd->rkgd/dot_general | solution.py:83
  164.1 0.8 constant_dynamic-slice_fusion.2
  165.2 7.6 %fusion.89 = (f32[8,384]{1,0:T(8,128)S(1)}, f32[1024,384,8]{1,0,2:T(8,128)}) fusion(pred[384,1024]{0,1:T(8,128)(4,1)S(1)} %broadcast_compare_fusion.3, bf16[384,1,8,128]{3,0,2,1:T(8,128)(2,1)S(1)} %get-tuple-element.236, bf16[6,1024,128]{2,1,0:T(8,128)(2,1)} %get-tuple-element.235, s32[]{:T(128)S(6)} %copy.105), kind=kOutput, calls=%fused_computation.3.clone.1 | convolution fusion | flops 814740480 | bytes 14036996 | tf_op jit(solution)/shard_map/while/body/eval_jaxpr/rkgd,ckd->kgrc/dot_general | solution.py:74
  172.8 6.7 %fusion.91 = f32[8,384]{1,0:T(8,128)S(1)} fusion(f32[1024,384,8]{1,0,2:T(8,128)} %get-tuple-element.206, f32[8,384]{1,0:T(8,128)S(1)} %bitcast.256, pred[384,1024]{0,1:T(8,128)(4,1)S(1)} %broadcast_compare_fusion.3), kind=kLoop, calls=%fused_computation.5.clone.1 | loop fusion | flops 15725568 | bytes 13000704 | tf_op jit(solution)/shard_map/while/body/eval_jaxpr/reduce_sum | solution.py:82
  179.6 1.5 copy-done.1
  181.1 5.7 %bitcast_add_fusion.6 = f32[384,1,8,128]{0,3,2,1:T(8,128)} fusion(f32[384,1,8,128]{0,3,2,1:T(8,128)} %get-tuple-element.222, f32[1024,384,8]{1,0,2:T(8,128)S(1)} %copy-done.1, f32[8,384]{1,0:T(8,128)S(1)} %bitcast.257, pred[384,1024]{0,1:T(8,128)(4,1)S(1)} %broadcast_compare_fusion.3, f32[384,8]{0,1:T(8,128)S(1)} %get-tuple-element.207, ...), kind=kOutput, calls=%fused_computation.9.clone.1 | convolution fusion | flops 822214656 | bytes 16408581 | tf_op jit(solution)/shard_map/while/body/eval_jaxpr/kgrc,ckd->rkgd/dot_general | solution.py:83
  186.7 0.8 constant_dynamic-slice_fusion.2
  187.8 7.6 %fusion.89 = (f32[8,384]{1,0:T(8,128)S(1)}, f32[1024,384,8]{1,0,2:T(8,128)}) fusion(pred[384,1024]{0,1:T(8,128)(4,1)S(1)} %broadcast_compare_fusion.3, bf16[384,1,8,128]{3,0,2,1:T(8,128)(2,1)S(1)} %get-tuple-element.236, bf16[6,1024,128]{2,1,0:T(8,128)(2,1)} %get-tuple-element.235, s32[]{:T(128)S(6)} %copy.105), kind=kOutput, calls=%fused_computation.3.clone.1 | convolution fusion | flops 814740480 | bytes 14036996 | tf_op jit(solution)/shard_map/while/body/eval_jaxpr/rkgd,ckd->kgrc/dot_general | solution.py:74
  195.4 6.7 %fusion.91 = f32[8,384]{1,0:T(8,128)S(1)} fusion(f32[1024,384,8]{1,0,2:T(8,128)} %get-tuple-element.206, f32[8,384]{1,0:T(8,128)S(1)} %bitcast.256, pred[384,1024]{0,1:T(8,128)(4,1)S(1)} %broadcast_compare_fusion.3), kind=kLoop, calls=%fused_computation.5.clone.1 | loop fusion | flops 15725568 | bytes 13000704 | tf_op jit(solution)/shard_map/while/body/eval_jaxpr/reduce_sum | solution.py:82
  202.2 1.5 copy-done.1
  203.7 5.7 %bitcast_add_fusion.6 = f32[384,1,8,128]{0,3,2,1:T(8,128)} fusion(f32[384,1,8,128]{0,3,2,1:T(8,128)} %get-tuple-element.222, f32[1024,384,8]{1,0,2:T(8,128)S(1)} %copy-done.1, f32[8,384]{1,0:T(8,128)S(1)} %bitcast.257, pred[384,1024]{0,1:T(8,128)(4,1)S(1)} %broadcast_compare_fusion.3, f32[384,8]{0,1:T(8,128)S(1)} %get-tuple-element.207, ...), kind=kOutput, calls=%fused_computation.9.clone.1 | convolution fusion | flops 822214656 | bytes 16408581 | tf_op jit(solution)/shard_map/while/body/eval_jaxpr/kgrc,ckd->rkgd/dot_general | solution.py:83
  209.4 0.8 constant_dynamic-slice_fusion.2
  210.4 7.6 %fusion.89 = (f32[8,384]{1,0:T(8,128)S(1)}, f32[1024,384,8]{1,0,2:T(8,128)}) fusion(pred[384,1024]{0,1:T(8,128)(4,1)S(1)} %broadcast_compare_fusion.3, bf16[384,1,8,128]{3,0,2,1:T(8,128)(2,1)S(1)} %get-tuple-element.236, bf16[6,1024,128]{2,1,0:T(8,128)(2,1)} %get-tuple-element.235, s32[]{:T(128)S(6)} %copy.105), kind=kOutput, calls=%fused_computation.3.clone.1 | convolution fusion | flops 814740480 | bytes 14036996 | tf_op jit(solution)/shard_map/while/body/eval_jaxpr/rkgd,ckd->kgrc/dot_general | solution.py:74
  218.0 6.7 %fusion.91 = f32[8,384]{1,0:T(8,128)S(1)} fusion(f32[1024,384,8]{1,0,2:T(8,128)} %get-tuple-element.206, f32[8,384]{1,0:T(8,128)S(1)} %bitcast.256, pred[384,1024]{0,1:T(8,128)(4,1)S(1)} %broadcast_compare_fusion.3), kind=kLoop, calls=%fused_computation.5.clone.1 | loop fusion | flops 15725568 | bytes 13000704 | tf_op jit(solution)/shard_map/while/body/eval_jaxpr/reduce_sum | solution.py:82
  224.8 1.5 copy-done.1
  226.3 5.7 %bitcast_add_fusion.6 = f32[384,1,8,128]{0,3,2,1:T(8,128)} fusion(f32[384,1,8,128]{0,3,2,1:T(8,128)} %get-tuple-element.222, f32[1024,384,8]{1,0,2:T(8,128)S(1)} %copy-done.1, f32[8,384]{1,0:T(8,128)S(1)} %bitcast.257, pred[384,1024]{0,1:T(8,128)(4,1)S(1)} %broadcast_compare_fusion.3, f32[384,8]{0,1:T(8,128)S(1)} %get-tuple-element.207, ...), kind=kOutput, calls=%fused_computation.9.clone.1 | convolution fusion | flops 822214656 | bytes 16408581 | tf_op jit(solution)/shard_map/while/body/eval_jaxpr/kgrc,ckd->rkgd/dot_general | solution.py:83
  232.0 0.8 constant_dynamic-slice_fusion.2
  233.0 7.6 %fusion.89 = (f32[8,384]{1,0:T(8,128)S(1)}, f32[1024,384,8]{1,0,2:T(8,128)}) fusion(pred[384,1024]{0,1:T(8,128)(4,1)S(1)} %broadcast_compare_fusion.3, bf16[384,1,8,128]{3,0,2,1:T(8,128)(2,1)S(1)} %get-tuple-element.236, bf16[6,1024,128]{2,1,0:T(8,128)(2,1)} %get-tuple-element.235, s32[]{:T(128)S(6)} %copy.105), kind=kOutput, calls=%fused_computation.3.clone.1 | convolution fusion | flops 814740480 | bytes 14036996 | tf_op jit(solution)/shard_map/while/body/eval_jaxpr/rkgd,ckd->kgrc/dot_general | solution.py:74
  240.6 6.7 %fusion.91 = f32[8,384]{1,0:T(8,128)S(1)} fusion(f32[1024,384,8]{1,0,2:T(8,128)} %get-tuple-element.206, f32[8,384]{1,0:T(8,128)S(1)} %bitcast.256, pred[384,1024]{0,1:T(8,128)(4,1)S(1)} %broadcast_compare_fusion.3), kind=kLoop, calls=%fused_computation.5.clone.1 | loop fusion | flops 15725568 | bytes 13000704 | tf_op jit(solution)/shard_map/while/body/eval_jaxpr/reduce_sum | solution.py:82
  247.4 1.5 copy-done.1
  248.9 5.7 %bitcast_add_fusion.6 = f32[384,1,8,128]{0,3,2,1:T(8,128)} fusion(f32[384,1,8,128]{0,3,2,1:T(8,128)} %get-tuple-element.222, f32[1024,384,8]{1,0,2:T(8,128)S(1)} %copy-done.1, f32[8,384]{1,0:T(8,128)S(1)} %bitcast.257, pred[384,1024]{0,1:T(8,128)(4,1)S(1)} %broadcast_compare_fusion.3, f32[384,8]{0,1:T(8,128)S(1)} %get-tuple-element.207, ...), kind=kOutput, calls=%fused_computation.9.clone.1 | convolution fusion | flops 822214656 | bytes 16408581 | tf_op jit(solution)/shard_map/while/body/eval_jaxpr/kgrc,ckd->rkgd/dot_general | solution.py:83
  254.6 0.8 constant_dynamic-slice_fusion.2
  255.6 7.6 %fusion.89 = (f32[8,384]{1,0:T(8,128)S(1)}, f32[1024,384,8]{1,0,2:T(8,128)}) fusion(pred[384,1024]{0,1:T(8,128)(4,1)S(1)} %broadcast_compare_fusion.3, bf16[384,1,8,128]{3,0,2,1:T(8,128)(2,1)S(1)} %get-tuple-element.236, bf16[6,1024,128]{2,1,0:T(8,128)(2,1)} %get-tuple-element.235, s32[]{:T(128)S(6)} %copy.105), kind=kOutput, calls=%fused_computation.3.clone.1 | convolution fusion | flops 814740480 | bytes 14036996 | tf_op jit(solution)/shard_map/while/body/eval_jaxpr/rkgd,ckd->kgrc/dot_general | solution.py:74
  263.2 6.7 %fusion.91 = f32[8,384]{1,0:T(8,128)S(1)} fusion(f32[1024,384,8]{1,0,2:T(8,128)} %get-tuple-element.206, f32[8,384]{1,0:T(8,128)S(1)} %bitcast.256, pred[384,1024]{0,1:T(8,128)(4,1)S(1)} %broadcast_compare_fusion.3), kind=kLoop, calls=%fused_computation.5.clone.1 | loop fusion | flops 15725568 | bytes 13000704 | tf_op jit(solution)/shard_map/while/body/eval_jaxpr/reduce_sum | solution.py:82
  270.0 1.5 copy-done.1
  271.5 5.7 %bitcast_add_fusion.6 = f32[384,1,8,128]{0,3,2,1:T(8,128)} fusion(f32[384,1,8,128]{0,3,2,1:T(8,128)} %get-tuple-element.222, f32[1024,384,8]{1,0,2:T(8,128)S(1)} %copy-done.1, f32[8,384]{1,0:T(8,128)S(1)} %bitcast.257, pred[384,1024]{0,1:T(8,128)(4,1)S(1)} %broadcast_compare_fusion.3, f32[384,8]{0,1:T(8,128)S(1)} %get-tuple-element.207, ...), kind=kOutput, calls=%fused_computation.9.clone.1 | convolution fusion | flops 822214656 | bytes 16408581 | tf_op jit(solution)/shard_map/while/body/eval_jaxpr/kgrc,ckd->rkgd/dot_general | solution.py:83
  277.2 1.5 divide_convert_fusion
  278.7 1.2 copy.88
  281.7 1.6 collective-permute-start.3
  283.3 4.4 %collective-permute-start.4 = (bf16[8,4,1,8]{3,1,0,2:T(4,128)(2,1)S(1)}, bf16[8,4,1,8]{3,1,0,2:T(4,128)(2,1)S(1)}, u32[]{:S(2)}, u32[]{:S(2)}) collective-permute-start(bf16[8,4,1,8]{3,1,0,2:T(4,128)(2,1)S(1)} %reduce_max.55), channel_id=1, source_target_pairs={{0,1},{1,0},{2,3},{3,2},{4,5},{5,4},{6,7},{7,6},{8,9},{9,8},{10,11... | collective-permute-start | bytes 1544 | tf_op jit(solution)/shard_map/ppermute | solution.py:40
  287.9 1.5 collective-permute-start.5
  289.7 4.5 %collective-permute-start.6 = (bf16[8,8,1,256]{3,1,0,2:T(8,128)(2,1)S(1)}, bf16[8,8,1,256]{3,1,0,2:T(8,128)(2,1)S(1)}, u32[]{:S(2)}, u32[]{:S(2)}) collective-permute-start(bf16[8,8,1,256]{3,1,0,2:T(8,128)(2,1)S(1)} %bitcast.279), channel_id=1, source_target_pairs={{0,1},{1,0},{2,3},{3,2},{4,5},{5,4},{6,7},{7,6},{8,9},{9,8},{10,11... | collective-permute-start | bytes 98312 | tf_op jit(solution)/shard_map/ppermute | solution.py:40
  294.3 1.2 collective-permute-done.5
  295.5 2.2 collective-permute-done.6
  (129 shorter events, 13.6 us)
Async XLA Ops:
  7.2 291.1 %copy-start = (bf16[1,8,4,128]{3,2,1,0:T(4,128)(2,1)S(1)}, bf16[1,8,4,128]{3,2,1,0:T(4,128)(2,1)}, u32[]{:S(2)}) copy-start(bf16[1,8,4,128]{3,2,1,0:T(4,128)(2,1)} %param.16) | copy-start | bytes 24580
  7.2 94.7 %copy-start.9 = (bf16[1,8,4,1024]{3,2,1,0:T(4,128)(2,1)S(1)}, bf16[1,8,4,1024]{3,2,1,0:T(4,128)(2,1)}, u32[]{:S(2)}) copy-start(bf16[1,8,4,1024]{3,2,1,0:T(4,128)(2,1)} %param.14) | copy-start | bytes 196612
  7.2 66.0 %copy-start.4 = (bf16[1,384,128]{2,1,0:T(8,128)(2,1)S(1)}, bf16[1,384,128]{2,1,0:T(8,128)(2,1)}, u32[]{:S(2)}) copy-start(bf16[1,384,128]{2,1,0:T(8,128)(2,1)} %param.13) | copy-start | bytes 294916
  7.2 94.8 %copy-start.6 = (bf16[1,384,1024]{2,1,0:T(8,128)(2,1)S(1)}, bf16[1,384,1024]{2,1,0:T(8,128)(2,1)}, u32[]{:S(2)}) copy-start(bf16[1,384,1024]{2,1,0:T(8,128)(2,1)} %param.11) | copy-start | bytes 2359300
  7.2 129.1 %all-gather.3.cloned.1.call-start = ((), (), s32[]{:S(2)}) async-start(), calls=%async_computation.4 | async-start | bytes 1966080 | tf_op jit(solution)/shard_map/all_gather | solution.py:28
  25.1 35.4 %collective-permute-start.2 = (bf16[8,4,1024]{2,1,0:T(4,128)(2,1)}, bf16[8,4,1024]{2,1,0:T(4,128)(2,1)S(1)}, u32[]{:S(2)}, u32[]{:S(2)}) collective-permute-start(bf16[8,4,1024]{2,1,0:T(4,128)(2,1)} %bitcast.277), channel_id=1, source_target_pairs={{0,1},{1,0},{2,3},{3,2},{4,5},{5,4},{6,7},{7,6},{8,9},{9,8},{10,11... | collective-permute-start | bytes 196616 | tf_op jit(solution)/shard_map/ppermute | solution.py:40
  30.0 7.6 %collective-permute-start.1 = (s32[8]{0:T(128)}, s32[8]{0:T(128)S(1)}, u32[]{:S(2)}, u32[]{:S(2)}) collective-permute-start(s32[8]{0:T(128)} %bitcast.281), channel_id=1, source_target_pairs={{0,1},{1,0},{2,3},{3,2},{4,5},{5,4},{6,7},{7,6},{8,9},{9,8},{10,11... | collective-permute-start | bytes 104 | tf_op jit(solution)/shard_map/ppermute | solution.py:40
  38.2 14.8 %all-to-all-start.1 = ((s32[16,1,8]{2,1,0:T(1,128)}), s32[16,1,8]{2,1,0:T(1,128)S(1)}, u32[]{:S(2)}, u32[]{:S(2)}) async-start(s32[16,1,8]{2,1,0:T(1,128)} %broadcast_in_dim.103), calls=%async_computation.1 | async-start | bytes 16384 | tf_op jit(solution)/shard_map/all_to_all | solution.py:45
  44.5 7.7 %collective-permute-start = (s32[8,16]{1,0:T(8,128)}, s32[8,16]{1,0:T(8,128)S(1)}, u32[]{:S(2)}, u32[]{:S(2)}) collective-permute-start(s32[8,16]{1,0:T(8,128)} %bitcast.280), channel_id=1, source_target_pairs={{0,1},{1,0},{2,3},{3,2},{4,5},{5,4},{6,7},{7,6},{8,9},{9,8},{10,11... | collective-permute-start | bytes 1544 | tf_op jit(solution)/shard_map/ppermute | solution.py:40
  52.9 14.0 %all-to-all-start = ((s32[16,1,128]{2,1,0:T(1,128)}), s32[16,1,128]{2,1,0:T(1,128)S(1)}, u32[]{:S(2)}, u32[]{:S(2)}) async-start(s32[16,1,128]{2,1,0:T(1,128)} %reshape.374), calls=%async_computation | async-start | bytes 16384 | tf_op jit(solution)/shard_map/all_to_all | solution.py:45
  68.1 34.7 %copy-start.10 = (bf16[8,128]{1,0:T(8,128)(2,1)S(1)}, bf16[8,128]{1,0:T(8,128)(2,1)}, u32[]{:S(2)}) copy-start(bf16[8,128]{1,0:T(8,128)(2,1)} %param.19) | copy-start | bytes 6148
  68.1 35.4 %copy-start.13 = (bf16[1,8,4,128]{3,2,1,0:T(4,128)(2,1)S(1)}, bf16[1,8,4,128]{3,2,1,0:T(4,128)(2,1)}, u32[]{:S(2)}) copy-start(bf16[1,8,4,128]{3,2,1,0:T(4,128)(2,1)} %param.15) | copy-start | bytes 24580
  68.1 42.7 %all-to-all-start.2 = ((bf16[16,8,4,1024]{3,1,2,0:T(8,128)(2,1)}), bf16[16,8,4,1024]{3,1,2,0:T(8,128)(2,1)S(1)}, u32[]{:S(2)}, u32[]{:S(2)}) async-start(bf16[16,8,4,1024]{3,1,2,0:T(8,128)(2,1)} %broadcast_in_dim.105), calls=%async_computation.2 | async-start | bytes 2097152 | tf_op jit(solution)/shard_map/all_to_all | solution.py:45
  73.1 35.1 %copy-start.3 = (bf16[1,384,128]{2,1,0:T(8,128)(2,1)S(1)}, bf16[1,384,128]{2,1,0:T(8,128)(2,1)}, u32[]{:S(2)}) copy-start(bf16[1,384,128]{2,1,0:T(8,128)(2,1)} %param.12) | copy-start | bytes 294916
  73.1 65.9 %all-gather.5.cloned.1.call-start = ((), (), s32[]{:S(2)}) async-start(), calls=%async_computation.5 | async-start | bytes 1966080 | tf_op jit(solution)/shard_map/all_gather | solution.py:28
  102.8 3.0 copy-start.11
  107.5 0.7 copy-start.7
  115.3 5.5 %copy-start.5 = (bf16[1,384,128]{2,1,0:T(8,128)(2,1)S(1)}, bf16[1,384,128]{2,1,0:T(8,128)(2,1)}, u32[]{:S(2)}) copy-start(bf16[1,384,128]{2,1,0:T(8,128)(2,1)} %param.13) | copy-start | bytes 294916
  120.8 3.1 %copy-start.2 = (bf16[128,4,1,8,384]{0,4,3,1,2:T(8,128)(2,1)S(1)}, bf16[128,4,1,8,384]{0,4,3,1,2:T(8,128)(2,1)}, u32[]{:S(2)}) copy-start(bf16[128,4,1,8,384]{0,4,3,1,2:T(8,128)(2,1)} %get-tuple-element.135) | copy-start | bytes 9437188
  129.0 150.9 %all-to-all-start.3 = ((bf16[16,8,6208]{2,1,0:T(8,128)(2,1)}), bf16[16,8,6208]{2,1,0:T(8,128)(2,1)S(1)}, u32[]{:S(2)}, u32[]{:S(2)}) async-start(bf16[16,8,6208]{2,1,0:T(8,128)(2,1)} %concatenate.14), calls=%async_computation.3 | async-start | bytes 3211264 | tf_op jit(solution)/shard_map/all_to_all | solution.py:59
  150.4 8.3 %copy-start.1 = (f32[1024,384,8]{1,0,2:T(8,128)S(1)}, f32[1024,384,8]{1,0,2:T(8,128)}, u32[]{:S(2)}) copy-start(f32[1024,384,8]{1,0,2:T(8,128)} %get-tuple-element.206) | copy-start | bytes 37748740 | tf_op jit(solution)/shard_map/while
  172.8 8.3 %copy-start.1 = (f32[1024,384,8]{1,0,2:T(8,128)S(1)}, f32[1024,384,8]{1,0,2:T(8,128)}, u32[]{:S(2)}) copy-start(f32[1024,384,8]{1,0,2:T(8,128)} %get-tuple-element.206) | copy-start | bytes 37748740 | tf_op jit(solution)/shard_map/while
  195.4 8.3 %copy-start.1 = (f32[1024,384,8]{1,0,2:T(8,128)S(1)}, f32[1024,384,8]{1,0,2:T(8,128)}, u32[]{:S(2)}) copy-start(f32[1024,384,8]{1,0,2:T(8,128)} %get-tuple-element.206) | copy-start | bytes 37748740 | tf_op jit(solution)/shard_map/while
  218.0 8.3 %copy-start.1 = (f32[1024,384,8]{1,0,2:T(8,128)S(1)}, f32[1024,384,8]{1,0,2:T(8,128)}, u32[]{:S(2)}) copy-start(f32[1024,384,8]{1,0,2:T(8,128)} %get-tuple-element.206) | copy-start | bytes 37748740 | tf_op jit(solution)/shard_map/while
  240.6 8.3 %copy-start.1 = (f32[1024,384,8]{1,0,2:T(8,128)S(1)}, f32[1024,384,8]{1,0,2:T(8,128)}, u32[]{:S(2)}) copy-start(f32[1024,384,8]{1,0,2:T(8,128)} %get-tuple-element.206) | copy-start | bytes 37748740 | tf_op jit(solution)/shard_map/while
  263.2 8.3 %copy-start.1 = (f32[1024,384,8]{1,0,2:T(8,128)S(1)}, f32[1024,384,8]{1,0,2:T(8,128)}, u32[]{:S(2)}) copy-start(f32[1024,384,8]{1,0,2:T(8,128)} %get-tuple-element.206) | copy-start | bytes 37748740 | tf_op jit(solution)/shard_map/while
  280.6 13.6 %copy-start.8 = (f32[8,4,1,8,4]{3,4,1,0,2:T(4,128)S(1)}, f32[8,4,1,8,4]{3,4,1,0,2:T(4,128)}, u32[]{:S(2)}) copy-start(f32[8,4,1,8,4]{3,4,1,0,2:T(4,128)} %get-tuple-element.144) | copy-start | bytes 12292
  280.6 13.6 %copy-start.12 = (pred[4,4]{1,0:T(4,128)(4,1)S(1)}, pred[4,4]{1,0:T(4,128)(4,1)}, u32[]{:S(2)}) copy-start(pred[4,4]{1,0:T(4,128)(4,1)} %copy-done.11) | copy-start | bytes 52
  281.7 16.6 %collective-permute-start.3 = (bf16[8,4,1,8,128]{4,3,1,0,2:T(8,128)(2,1)S(1)}, bf16[8,4,1,8,128]{4,3,1,0,2:T(8,128)(2,1)S(1)}, u32[]{:S(2)}, u32[]{:S(2)}) collective-permute-start(bf16[8,4,1,8,128]{4,3,1,0,2:T(8,128)(2,1)S(1)} %bitcast.278), channel_id=1, source_target_pairs={{0,1},{1,0},{2,3},{3,2},{4,5},{5,4},{6,7},{7,6},{8,9},{9,8},{10,11... | collective-permute-start | bytes 196616 | tf_op jit(solution)/shard_map/ppermute | solution.py:40
  283.3 10.9 %collective-permute-start.4 = (bf16[8,4,1,8]{3,1,0,2:T(4,128)(2,1)S(1)}, bf16[8,4,1,8]{3,1,0,2:T(4,128)(2,1)S(1)}, u32[]{:S(2)}, u32[]{:S(2)}) collective-permute-start(bf16[8,4,1,8]{3,1,0,2:T(4,128)(2,1)S(1)} %reduce_max.55), channel_id=1, source_target_pairs={{0,1},{1,0},{2,3},{3,2},{4,5},{5,4},{6,7},{7,6},{8,9},{9,8},{10,11... | collective-permute-start | bytes 1544 | tf_op jit(solution)/shard_map/ppermute | solution.py:40
  287.9 7.6 %collective-permute-start.5 = (bf16[8,4,1,8]{3,1,0,2:T(4,128)(2,1)S(1)}, bf16[8,4,1,8]{3,1,0,2:T(4,128)(2,1)S(1)}, u32[]{:S(2)}, u32[]{:S(2)}) collective-permute-start(bf16[8,4,1,8]{3,1,0,2:T(4,128)(2,1)S(1)} %convert_element_type.210), channel_id=1, source_target_pairs={{0,1},{1,0},{2,3},{3,2},{4,5},{5,4},{6,7},{7,6},{8,9},{9,8},{10,11... | collective-permute-start | bytes 1544 | tf_op jit(solution)/shard_map/ppermute | solution.py:40
  289.7 8.0 %collective-permute-start.6 = (bf16[8,8,1,256]{3,1,0,2:T(8,128)(2,1)S(1)}, bf16[8,8,1,256]{3,1,0,2:T(8,128)(2,1)S(1)}, u32[]{:S(2)}, u32[]{:S(2)}) collective-permute-start(bf16[8,8,1,256]{3,1,0,2:T(8,128)(2,1)S(1)} %bitcast.279), channel_id=1, source_target_pairs={{0,1},{1,0},{2,3},{3,2},{4,5},{5,4},{6,7},{7,6},{8,9},{9,8},{10,11... | collective-permute-start | bytes 98312 | tf_op jit(solution)/shard_map/ppermute | solution.py:40
Sparse Core Ops, SparseCore 0:
  25.2 28.5 all-gather.2
  102.0 26.6 all-gather.4
where the time goes:
time: 307 us; the launch traced here: 306 us
  matrix products  91 us (30%)
  other arithmetic  52.8 us (17%)
  blocking collectives  46.5 us (15%)
  starting transfers between devices  45.9 us (15%)
  local copies, waits for them, and re-layouts  32.7 us (11%)
  waiting for transfers between devices  22.5 us (7%)
  between operations  14.5 us (5%)
    all_gather x2, blocking collectives, gather_in_order(): parts = lax.all_gather(parts, axes[k], axis=0, tiled=True)  46.5 us
    dot_general x6, matrix products, fold_block(): jnp.einsum('rkgd,ckd->kgrc', query_heads, key_heads, preferred_element_ty...  45.6 us
    reduce_sum x6, other arithmetic, fold_block(): totals = totals * fading + jnp.sum(weights, axis=-1)  40.5 us
    dot_general x6, matrix products, fold_block(): jnp.einsum('kgrc,ckd->rkgd', weights.astype(jnp.bfloat16), value_heads, p...  33.8 us
    ppermute x7, starting transfers between devices, partner(): lax.ppermute(shard, axis, [(i, i ^ 1 << apart) for i in range(lax.axis_si...  19.6 us
    all_to_all x3, starting transfers between devices, from_everyone(): lax.all_to_all(jnp.broadcast_to(shard[None], (peers, *shard.shape)), axis...  18.9 us
    ppermute x7, waiting for transfers between devices, partner(): lax.ppermute(shard, axis, [(i, i ^ 1 << apart) for i in range(lax.axis_si...  16 us
    while x18, local copies, waits for them, and re-layouts  8.92 us
  transfers between devices with their start and end apart: 13, of which 5 were waited for; matrix products, arithmetic and copies ran while one was open for 54% of the time, Pallas kernels for 0%

commit v1 on v0

v1 whole, which is shorter than its diff:
```python
import math

import jax
import jax.numpy as jnp
from jax import lax
from jax.experimental import pallas as pl
from jax.experimental.pallas import tpu as pltpu
from jax.sharding import Mesh
from jax.sharding import PartitionSpec as P


HD = 128
PAGE = 128
ROWS = 384
HEADS = 8
REQ = 8
STEPS = 4
SLOTS = 16
CSW = 8
QROWS = HEADS * REQ * STEPS
SCALE = math.log2(math.e) / math.sqrt(HD)
LOW = -1e30
LARGE = 2.0**100
SEQ = ("z", "x")
STATE = (HEADS, ROWS, HD)
PAIR = 2

f32 = jnp.float32
bf16 = jnp.bfloat16


def dot_t(a, b):
    return lax.dot_general(a, b, (((1,), (1,)), ((), ())), preferred_element_type=f32)


def dot(a, b):
    return lax.dot_general(a, b, (((1,), (0,)), ((), ())), preferred_element_type=f32)


SMALL = pltpu.CompilerParams(vmem_limit_bytes=8 << 20)


def smem():
    return pl.BlockSpec(memory_space=pltpu.SMEM)


def prepare_body(length, query, table, new_keys, new_values, out, m_out, l_out, a_out, wide):
    for g in range(HEADS):
        out[g * 32 : (g + 1) * 32, :] = query[:, :, g * HD : (g + 1) * HD].astype(f32).reshape(32, HD).astype(bf16)
    wide[...] = jnp.zeros((REQ, HD), jnp.int32)
    wide[:, :SLOTS] = table[...]
    lane = lax.broadcasted_iota(jnp.int32, (REQ, HD), 1)
    line = lax.broadcasted_iota(jnp.int32, (REQ, HD), 0)
    tokens = jnp.zeros((REQ, HD), jnp.int32)
    for r in range(REQ):
        tokens = jnp.where(line == r, length[0, r], tokens)
    limit = jnp.clip(tokens - (lane - SLOTS) * PAGE, 0, PAGE)
    facts = jnp.where(lane < SLOTS, wide[...], jnp.where(lane < 2 * SLOTS, limit, 0))
    facts = jnp.concatenate([facts.astype(f32), jnp.zeros((8, HD), f32)], axis=0)
    out[QROWS:, :] = facts.astype(bf16)
    s = dot_t(out[:QROWS, :], new_keys[...]) * SCALE
    row = lax.broadcasted_iota(jnp.int32, (QROWS, 32), 0) % 32
    col = lax.broadcasted_iota(jnp.int32, (QROWS, 32), 1)
    seen = (row // STEPS == col // STEPS) & (col <= row)
    s = jnp.where(seen, s, LOW)
    top = jnp.max(s, axis=1, keepdims=True)
    w = jnp.exp2(s - top)
    m_out[...] = jnp.broadcast_to(top, (QROWS, HD))
    l_out[...] = jnp.broadcast_to(jnp.sum(w, axis=1, keepdims=True), (QROWS, HD))
    a_out[...] = dot(w.astype(bf16), new_values[...])


def prepare(query, table, length, new_keys, new_values):
    vmem = pl.BlockSpec(memory_space=pltpu.VMEM)
    return pl.pallas_call(
        prepare_body,
        in_specs=[smem()] + [vmem] * 4,
        out_specs=(vmem,) * 4,
        out_shape=(jax.ShapeDtypeStruct((QROWS + 16, HD), bf16),) + (jax.ShapeDtypeStruct((QROWS, HD), f32),) * 3,
        scratch_shapes=[pltpu.VMEM((REQ, HD), jnp.int32)],
        compiler_params=SMALL,
        name="prepare",
    )(length, query, table, new_keys, new_values)


class Block:
    def __init__(self, key_ref, key_col, value_ref, value_col, n=None):
        self.parts = ((key_ref, key_col), (value_ref, value_col))
        self.n = n

    def rows(self, which, start, stop):
        ref, col = self.parts[which]
        if self.n is None:
            return ref[start:stop, col * HD : (col + 1) * HD]
        return ref[self.n, start:stop, col * HD : (col + 1) * HD]

    def key(self):
        return self.rows(0, 0, ROWS)

    def value(self):
        return self.rows(1, 0, ROWS)


def chunks_of(blocks):
    half = [(b, i * HD) for b in blocks for i in range(ROWS // HD)]
    for i in range(0, len(half), 2):
        some = half[i : i + 2]
        yield tuple(
            jnp.concatenate([b.rows(which, r, r + HD) for b, r in some], axis=0) for which in (0, 1)
        )


def fold_fixed(before, after, h, q, blocks):
    level = before[0][h]
    total = before[1][h]
    mixed = before[2][h]
    for k, v in chunks_of(blocks):
        scores = dot_t(q(), k)
        weights = [jnp.exp2(scores[:, i : i + HD] * SCALE - level) for i in range(0, scores.shape[1], HD)]
        for w in weights:
            total = total + w
        mixed = mixed + dot(jnp.concatenate([w.astype(bf16) for w in weights], axis=1), v)
    after[1][h] = total
    after[2][h] = mixed


def fold_moving(before, after, h, q, blocks):
    m_ref, l_ref, a_ref = after

    @pl.loop(0, ROWS // HD)
    def _(i):
        rows = pl.ds(pl.multiple_of(i * HD, HD), HD)
        l_ref[h, rows] = before[1][h, rows]
        a_ref[h, rows] = before[2][h, rows]
        for b in blocks:
            scores = dot_t(q(rows), b.key()) * SCALE
            level = m_ref[h, rows]
            now = jnp.maximum(level, jnp.max(scores, axis=1, keepdims=True))
            fade = jnp.exp2(level - now)
            weights = [jnp.exp2(scores[:, j : j + HD] - now) for j in range(0, ROWS, HD)]
            m_ref[h, rows] = now
            l_ref[h, rows] = l_ref[h, rows] * fade + (weights[0] + weights[1] + weights[2])
            update = dot(jnp.concatenate([w.astype(bf16) for w in weights], axis=1), b.value())
            a_ref[h, rows] = a_ref[h, rows] * fade + update


def too_large(l_ref):
    top = l_ref[0]
    for h in range(1, HEADS):
        top = jnp.maximum(top, l_ref[h])
    return jnp.max(top) > LARGE


def fold_own(state, h, q, own):
    m_ref, l_ref, a_ref = state
    scores = dot_t(q(), own.key()) * SCALE
    row = lax.broadcasted_iota(jnp.int32, (ROWS, ROWS), 0)
    col = lax.broadcasted_iota(jnp.int32, (ROWS, ROWS), 1)
    scores = jnp.where(col <= row, scores, LOW)
    now = jnp.max(scores, axis=1, keepdims=True)
    weights = jnp.exp2(scores - now)
    m_ref[h] = jnp.broadcast_to(now, (ROWS, HD))
    l_ref[h] = weights[:, :HD] + weights[:, HD : 2 * HD] + weights[:, 2 * HD :]
    a_ref[h] = dot(weights.astype(bf16), own.value())


def cost(blocks):
    n = HEADS * ROWS * ROWS * blocks
    return pl.CostEstimate(flops=4 * n * HD, bytes_accessed=1 << 20, transcendentals=n)


def part(groups, place, query, arrays, state=None, last=False, own=None, weight=4):
    count = len(arrays)
    carried = [] if state is None else list(state)

    def body(place_ref, q_ref, *refs):
        blocks = refs[:count]
        before = refs[count : count + len(carried)]
        after = refs[count + len(carried) :]
        out = None
        if last:
            out, after = after[0], (before[0],) + tuple(after[1:])
        cases = groups(blocks)
        z, x = place_ref[0], place_ref[1]

        def query_of(h):
            lanes = pl.ds(pl.multiple_of(h * HD, HD), HD)
            return lambda rows=slice(None): q_ref[rows, lanes]

        def run(folded, slow):
            if own is not None:

                @pl.loop(0, HEADS // PAIR)
                def _(i):
                    for n in range(PAIR):
                        h = i * PAIR + n
                        fold_own(after, h, query_of(h), own(blocks))

            source = after if own is not None else before
            idle = None
            for holds, step, some in cases:
                held = holds(z, x)
                idle = held if idle is None else idle | held
                if slow:
                    step = 1

                @pl.when(held)
                def _(some=some, step=step):
                    @pl.loop(0, HEADS // step)
                    def _(i):
                        for n in range(step):
                            h = i * step + n
                            folded(source, after, h, query_of(h), some)

            if own is None:

                @pl.when(jnp.logical_not(idle))
                def _():
                    @pl.loop(0, HEADS)
                    def _(h):
                        after[1][h] = before[1][h]
                        after[2][h] = before[2][h]

        run(fold_fixed, False)

        @pl.when(too_large(after[1]))
        def _():
            run(fold_moving, True)

        if last:

            @pl.loop(0, HEADS)
            def _(h):
                total = jnp.sum(after[1][h], axis=1, keepdims=True)
                out[:, pl.ds(pl.multiple_of(h * HD, HD), HD)] = (after[2][h] / total).astype(bf16)

    vmem = pl.BlockSpec(memory_space=pltpu.VMEM)
    shape = jax.ShapeDtypeStruct(STATE, f32)
    if last:
        how = dict(
            out_specs=vmem,
            out_shape=jax.ShapeDtypeStruct((ROWS, HEADS * HD), bf16),
            scratch_shapes=[pltpu.VMEM(STATE, f32)] * 2,
        )
    else:
        how = dict(
            out_specs=(vmem,) * 3,
            out_shape=(shape,) * 3,
            input_output_aliases={2 + count: 0} if carried else {},
        )
    return pl.pallas_call(
        body,
        in_specs=[smem()] + [vmem] * (1 + count + len(carried)),
        compiler_params=pltpu.CompilerParams(vmem_limit_bytes=20 << 20),
        cost_estimate=cost(weight),
        **how,
    )(place, query, *arrays, *carried)


def count_body(ask, check, each_out, weighted_out, n_ref):
    facts = ask[QROWS : QROWS + 16, :].astype(f32)[:REQ]
    lane = lax.broadcasted_iota(jnp.int32, (REQ, HD), 1).astype(f32)
    named = [jnp.broadcast_to(facts[:, j : j + 1], (REQ, HD)) for j in range(SLOTS)]
    fits = [jnp.where(lane < facts[:, SLOTS + j : SLOTS + j + 1], 1.0, 0.0) for j in range(SLOTS)]
    checks = check[...].astype(f32)
    upper = lax.broadcasted_iota(jnp.int32, (8, HD), 0) < STEPS

    @pl.loop(0, 16)
    def _(b):
        for i in range(ROWS // PAGE):
            page = (b * (ROWS // PAGE) + i).astype(f32)
            n = jnp.zeros((REQ, HD), f32)
            for j in range(SLOTS):
                n = n + jnp.where(named[j] == page, fits[j], 0.0)
            n_ref[...] = n
            lines = [jnp.broadcast_to(n_ref[r : r + 1, :], (8, HD)) for r in range(REQ)]
            for r in range(0, REQ, 2):
                each_out[b, r * 4 : r * 4 + 8, i * HD : (i + 1) * HD] = jnp.where(upper, lines[r], lines[r + 1])
                both = jnp.concatenate([lines[r] * checks, lines[r + 1] * checks], axis=0)
                weighted_out[b, r * 8 : r * 8 + 16, i * HD : (i + 1) * HD] = both.astype(bf16)


def count_part(ask, check):
    return pl.pallas_call(
        count_body,
        out_shape=(
            jax.ShapeDtypeStruct((16, 32, ROWS), f32),
            jax.ShapeDtypeStruct((16, REQ * CSW, ROWS), bf16),
        ),
        scratch_shapes=[pltpu.VMEM((REQ, HD), f32)],
        compiler_params=SMALL,
        cost_estimate=pl.CostEstimate(flops=1 << 24, bytes_accessed=2 << 20, transcendentals=0),
        name="count",
    )(ask, check)


def context_body(blocks_of, count, place, ask, each_ref, weighted_ref, *refs):
    held = blocks_of(refs[:count])
    out, m_ref, l_ref, a_ref, s_ref = refs[count:]
    z, x = place[0], place[1]
    q = ask[:QROWS, :]

    def index(dz, dx):
        return ((z + 4 - dz) % 4) * 4 + (x + 4 - dx) % 4

    def apply(dz, dx, block):
        b = index(dz, dx)
        scores = dot_t(q, block.key()) * SCALE
        each = jnp.concatenate([each_ref[b]] * HEADS, axis=0)
        return b, scores, each

    level = jnp.max(dot_t(q, held[0][2].key()), axis=1, keepdims=True) * SCALE
    level = jnp.maximum(jnp.full((QROWS, HD), LOW), level)
    total = jnp.zeros((QROWS, HD), f32)
    mixed = jnp.zeros((QROWS + REQ * CSW, HD), f32)
    digest_k = jnp.zeros((REQ * CSW, HD), f32)
    for dz, dx, block in held:
        b, scores, each = apply(dz, dx, block)
        weights = [
            jnp.exp2(scores[:, i : i + HD] - level) * each[:, i : i + HD] for i in range(0, ROWS, HD)
        ]
        total = total + (weights[0] + weights[1] + weights[2])
        weighted = weighted_ref[b]
        left = jnp.concatenate([jnp.concatenate([w.astype(bf16) for w in weights], axis=1), weighted], axis=0)
        mixed = mixed + dot(left, block.value())
        digest_k = digest_k + dot(weighted, block.key())
    m_ref[...] = level
    l_ref[...] = jnp.broadcast_to(jnp.sum(total, axis=1, keepdims=True), (QROWS, HD))
    a_ref[...] = mixed
    spread = l_ref[...]

    @pl.when(jnp.logical_not((jnp.max(spread) < LARGE) & (jnp.min(spread) > 1 / LARGE)))
    def _():
        @pl.loop(0, HEADS)
        def _(g):
            rows = pl.ds(pl.multiple_of(g * 32, 32), 32)
            top = jnp.full((32, HD), LOW)
            for n, (dz, dx, block) in enumerate(held):
                scores = dot_t(ask[rows, :], block.key()) * SCALE
                scores = jnp.where(each_ref[index(dz, dx)] > 0, scores, LOW)
                s_ref[n] = scores
                top = jnp.maximum(top, jnp.max(scores, axis=1, keepdims=True))
            total = jnp.zeros((32, HD), f32)
            mixed = jnp.zeros((32, HD), f32)
            for n, (dz, dx, block) in enumerate(held):
                weights = jnp.exp2(s_ref[n] - top[:, :1]) * each_ref[index(dz, dx)]
                total = total + jnp.sum(weights, axis=1, keepdims=True)
                mixed = mixed + dot(weights.astype(bf16), block.value())
            m_ref[rows, :] = top
            l_ref[rows, :] = total
            a_ref[rows, :] = mixed

    total = l_ref[...]
    out[:QROWS, :] = (a_ref[:QROWS, :] / total).astype(bf16)
    out[QROWS : QROWS + 64, :] = digest_k.astype(bf16)
    out[QROWS + 64 : QROWS + 128, :] = a_ref[QROWS:, :].astype(bf16)
    top = m_ref[...] + jnp.log2(total)
    diagonal = lax.broadcasted_iota(jnp.int32, (HD, HD), 0) == lax.broadcasted_iota(jnp.int32, (HD, HD), 1)
    line = lax.broadcasted_iota(jnp.int32, (16, HD), 0)
    packed = jnp.zeros((16, HD), f32)
    for i in range(2):
        rest = jnp.sum(jnp.where(diagonal, top[i * HD : (i + 1) * HD], 0.0), axis=0, keepdims=True)
        for n in range(3):
            piece = rest.astype(bf16).astype(f32)
            packed = jnp.where(line == 2 * n + i, jnp.broadcast_to(piece, (16, HD)), packed)
            rest = rest - piece
    out[QROWS + 128 :, :] = packed.astype(bf16)


def context_part(place, ask, each, weighted, arrays, blocks_of):
    vmem = pl.BlockSpec(memory_space=pltpu.VMEM)
    return pl.pallas_call(
        lambda *refs: context_body(blocks_of, len(arrays), *refs),
        in_specs=[smem()] + [vmem] * (3 + len(arrays)),
        out_specs=vmem,
        out_shape=jax.ShapeDtypeStruct((QROWS + 144, HD), bf16),
        scratch_shapes=[
            pltpu.VMEM((QROWS, HD), f32),
            pltpu.VMEM((QROWS, HD), f32),
            pltpu.VMEM((QROWS + REQ * CSW, HD), f32),
            pltpu.VMEM((16, 32, ROWS), f32),
        ],
        compiler_params=pltpu.CompilerParams(vmem_limit_bytes=20 << 20),
        cost_estimate=pl.CostEstimate(
            flops=4 * QROWS * 16 * ROWS * HD, bytes_accessed=4 << 20, transcendentals=QROWS * 16 * ROWS
        ),
        name="context",
    )(place, ask, each, weighted, *arrays)


def finish_body(back, m_ref, l_ref, a_ref, out, digest):
    diagonal = lax.broadcasted_iota(jnp.int32, (HD, HD), 0) == lax.broadcasted_iota(jnp.int32, (HD, HD), 1)
    tail = back[QROWS + 128 :, :].astype(f32)
    level = []
    for i in range(2):
        line = tail[i : i + 1] + tail[2 + i : 3 + i] + tail[4 + i : 5 + i]
        spread = jnp.where(diagonal, jnp.broadcast_to(line, (HD, HD)), 0.0)
        level.append(jnp.sum(spread, axis=1, keepdims=True))
    level = jnp.concatenate(level, axis=0)
    new = m_ref[...]
    joint = jnp.maximum(level, new)
    old = jnp.exp2(level - joint)
    new = jnp.exp2(new - joint)
    mixed = back[:QROWS, :].astype(f32) * old + a_ref[...] * new
    mixed = mixed / (old + l_ref[...] * new)
    for g in range(HEADS):
        out[:, :, g * HD : (g + 1) * HD] = mixed[g * 32 : (g + 1) * 32].reshape(REQ, STEPS, HD).astype(bf16)
    digest[:, :HD] = back[QROWS : QROWS + 64, :].astype(f32)
    digest[:, HD:] = back[QROWS + 64 : QROWS + 128, :].astype(f32)


def finish(back, fresh):
    return pl.pallas_call(
        finish_body,
        out_shape=(
            jax.ShapeDtypeStruct((REQ, STEPS, HEADS * HD), bf16),
            jax.ShapeDtypeStruct((REQ * CSW, 2 * HD), f32),
        ),
        compiler_params=SMALL,
        name="finish",
    )(back, *fresh)


def turn(shard, axis, by):
    n = lax.axis_size(axis)
    return lax.ppermute(shard, axis, [(i, (i + by) % n) for i in range(n)])


def swap(shard):
    return lax.ppermute(shard, "grp", [(0, 1), (1, 0)])


def work(
    prefill_query,
    prefill_keys,
    prefill_values,
    decode_query,
    decode_keys,
    decode_values,
    page_table,
    context_lengths,
    check_rows,
):
    place = jnp.stack([lax.axis_index("z"), lax.axis_index("x")]).astype(jnp.int32)
    query = prefill_query[0]
    own = jnp.concatenate([prefill_keys[0], prefill_values[0]], axis=1)
    up = [turn(own, "z", d) for d in (1, 2, 3)]
    right = turn(own, "x", 1)
    left = turn(own, "x", -1)
    asking = decode_query[0]
    ask, *fresh = prepare(
        asking, page_table[0], context_lengths, decode_keys[0].reshape(-1, HD), decode_values[0].reshape(-1, HD)
    )
    asked = swap(ask)

    def both(ref, n=None):
        return Block(ref, 0, ref, 1, n)

    state = part(
        lambda r: [
            (lambda z, x: x == 3, PAIR, [both(r[1]), both(r[2])]),
            (lambda z, x: (x >= 1) & (x < 3), PAIR, [both(r[1])]),
        ],
        place,
        query,
        [own, right, left],
        own=lambda r: both(r[0]),
        weight=3,
    )
    each, weighted = count_part(asked, check_rows)
    up = jnp.stack(up)
    up_right = turn(up, "x", 1)
    up_left = turn(up, "x", -1)
    far_k = turn(right[:, :HD], "x", 1)
    far_v = turn(left[:, HD:], "x", -1)

    def rising(r):
        ups = [both(r[0], n) for n in range(3)]
        far = [Block(r[1], 0, r[2], 0)]
        return [
            (lambda z, x: (z == 3) & (x >= 2), PAIR, ups + far),
            (lambda z, x: (z == 3) & (x < 2), 1, ups),
            (lambda z, x: (z == 2) & (x >= 2), 1, ups[:2] + far),
            (lambda z, x: (z == 2) & (x < 2), 1, ups[:2]),
            (lambda z, x: (z == 1) & (x >= 2), 1, ups[:1] + far),
            (lambda z, x: (z == 1) & (x < 2), 1, ups[:1]),
            (lambda z, x: (z == 0) & (x >= 2), 1, far),
        ]

    state = part(rising, place, query, [up, far_k, far_v], state)
    up_k = turn(up_right[:, :, :HD], "x", 1)
    up_v = turn(up_left[:, :, HD:], "x", -1)

    def beside(r, n):
        return [both(r[0], n), both(r[1], n)]

    state = part(
        lambda r: [(lambda z, x: z >= 2, PAIR, beside(r, 0) + beside(r, 1)), (lambda z, x: z == 1, 1, beside(r, 0))],
        place,
        query,
        [up_right, up_left],
        state,
    )

    def everything(r):
        own, right, left, far_k, far_v, up, up_right, up_left, up_k, up_v = r
        held = [(0, 0, both(own)), (0, 1, both(right)), (0, 3, both(left)), (0, 2, Block(far_k, 0, far_v, 0))]
        for n in range(3):
            held += [
                (n + 1, 0, both(up, n)),
                (n + 1, 1, both(up_right, n)),
                (n + 1, 3, both(up_left, n)),
                (n + 1, 2, Block(up_k, 0, up_v, 0, n)),
            ]
        return held

    back = context_part(
        place,
        asked,
        each,
        weighted,
        [own, right, left, far_k, far_v, up, up_right, up_left, up_k, up_v],
        everything,
    )
    returned = swap(back)

    def rest(r):
        far = [Block(r[2], 0, r[3], 0, n) for n in range(3)]
        return [
            (lambda z, x: z == 3, PAIR, beside(r, 2) + far),
            (lambda z, x: z == 2, 1, far[:2]),
            (lambda z, x: z == 1, 1, far[:1]),
        ]

    prefill_out = part(rest, place, query, [up_right, up_left, up_k, up_v], state, last=True, weight=5)
    decode_out, digest = finish(returned, fresh)
    return (
        prefill_out[None],
        decode_out.reshape(1, REQ, STEPS, HEADS * HD),
        digest.reshape(1, REQ, CSW, 2 * HD),
    )


def solution(mesh):
    split = Mesh(
        mesh.devices.reshape(4, 4, mesh.shape["tp"], mesh.shape["grp"]),
        ("z", "x", "tp", "grp"),
    )
    placed = (
        P("grp", SEQ, "tp"),
        P("grp", SEQ, "tp"),
        P("grp", SEQ, "tp"),
        P("grp", SEQ, None, "tp"),
        P("grp", SEQ, None, "tp"),
        P("grp", SEQ, None, "tp"),
        P("grp", SEQ, None),
        P("grp", SEQ),
        P(),
    )
    return jax.shard_map(
        work,
        mesh=split,
        in_specs=placed,
        out_specs=(P("grp", SEQ, "tp"), P("grp", SEQ, None, "tp"), P("grp", SEQ, None, "tp")),
        check_vma=False,
    )
```

time: 307 us -> 123 us (0.40)
  the two profiles are of different devices: /device:TPU:10 before, /device:TPU:114 now
where the time goes in v1:
time: 123 us
  Pallas kernels  72.7 us (59%)
  waiting for transfers between devices  25.1 us (20%)
  starting transfers between devices  21.7 us (18%)
  local copies, waits for them, and re-layouts  1.28 us (1%)
    pallas_call x4, Pallas kernels, part(): pl.pallas_call(body, in_specs=[smem()] + [vmem] * (1 + count + len(carrie...  65.3 us
    ppermute x11, waiting for transfers between devices, turn(): return lax.ppermute(shard, axis, [(i, (i + by) % n) for i in range(n)])  22.3 us
    ppermute x2, starting transfers between devices, swap(): return lax.ppermute(shard, 'grp', [(0, 1), (1, 0)])  11 us
    ppermute x11, starting transfers between devices, turn(): return lax.ppermute(shard, axis, [(i, (i + by) % n) for i in range(n)])  10.8 us
    pallas_call x1, Pallas kernels, context_part(): pl.pallas_call(lambda *refs: context_body(blocks_of, len(arrays), *refs),...  4.77 us
    ppermute x2, waiting for transfers between devices, swap(): return lax.ppermute(shard, 'grp', [(0, 1), (1, 0)])  2.83 us
  transfers between devices with their start and end apart: 13, of which 4 were waited for; matrix products, arithmetic and copies ran while one was open for 0% of the time, Pallas kernels for 55%

profile of v1, /device:TPU:114, one launch (start us, length us, event | category | flops | bytes accessed | tf_op | source)
XLA Modules:
  0.0 122.7 jit_solution(12670037297319769035)
XLA Ops:
  0.6 0.0 copy-start.3
  0.6 0.0 copy-start.1
  0.7 0.0 copy-start.2
  0.7 0.0 copy-start
  0.7 0.0 copy-start.5
  0.7 0.0 copy-start.4
  0.7 1.0 pad_maximum_fusion.1.refs_0_.refs_4_
  1.7 0.1 collective-permute-start
  1.8 1.6 %collective-permute-start.1 = (bf16[384,256]{1,0:T(8,128)(2,1)S(1)}, bf16[384,256]{1,0:T(8,128)(2,1)S(1)}, u32[]{:S(2)}, u32[]{:S(2)}) collective-permute-start(bf16[384,256]{1,0:T(8,128)(2,1)S(1)} %pad_maximum_fusion.1.refs_0_.refs_4_), channel_id=1, source_target_pairs={{0,128},{64,192},{128,0},{192,64},{1,129},{65,193},{129,1},{193,65... | collective-permute-start | bytes 589832 | tf_op jit(solution)/shard_map/ppermute | solution.py:426
  3.4 0.5 collective-permute-start.2
  3.8 5.0 %collective-permute-done = bf16[384,256]{1,0:T(8,128)(2,1)S(1)} collective-permute-done((bf16[384,256]{1,0:T(8,128)(2,1)S(1)}, bf16[384,256]{1,0:T(8,128)(2,1)S(1)}, u32[]{:S(2)}, u32[]{:S(2)}) %collective-permute-start) | collective-permute-done | bytes 196640 | tf_op jit(solution)/shard_map/ppermute | solution.py:426
  8.8 11.8 %collective-permute-done.1 = bf16[384,256]{1,0:T(8,128)(2,1)S(1)} collective-permute-done((bf16[384,256]{1,0:T(8,128)(2,1)S(1)}, bf16[384,256]{1,0:T(8,128)(2,1)S(1)}, u32[]{:S(2)}, u32[]{:S(2)}) %collective-permute-start.1) | collective-permute-done | bytes 196640 | tf_op jit(solution)/shard_map/ppermute | solution.py:426
  20.6 0.0 collective-permute-done.2
  20.6 0.1 pad_maximum_fusion.refs_0_.refs_9_
  20.7 1.6 %collective-permute-start.3 = (bf16[3,384,256]{2,1,0:T(8,128)(2,1)S(1)}, bf16[3,384,256]{2,1,0:T(8,128)(2,1)S(1)}, u32[]{:S(2)}, u32[]{:S(2)}) collective-permute-start(bf16[3,384,256]{2,1,0:T(8,128)(2,1)S(1)} %pad_maximum_fusion.refs_0_.refs_9_), channel_id=1, source_target_pairs={{0,16},{16,32},{32,48},{48,0},{1,17},{17,33},{33,49},{49,1},{2,18}... | collective-permute-start | bytes 1769480 | tf_op jit(solution)/shard_map/ppermute | solution.py:426
  22.3 0.5 collective-permute-start.4
  22.8 1.7 %collective-permute-start.9 = (bf16[384,256]{1,0:T(8,128)(2,1)S(1)}, bf16[384,256]{1,0:T(8,128)(2,1)S(1)}, u32[]{:S(2)}, u32[]{:S(2)}) collective-permute-start(bf16[384,256]{1,0:T(8,128)(2,1)S(1)} %pad_maximum_fusion.1.refs_0_.refs_4_), channel_id=1, source_target_pairs={{0,48},{16,0},{32,16},{48,32},{1,49},{17,1},{33,17},{49,33},{2,50}... | collective-permute-start | bytes 589832 | tf_op jit(solution)/shard_map/ppermute | solution.py:426
  24.5 0.3 collective-permute-start.7
  24.8 0.0 copy-done.3
  24.8 0.0 copy-done.1
  24.8 0.0 copy-done.2
  24.8 0.0 copy-done
  24.8 0.0 copy-done.5
  24.8 0.9 prepare.1
  25.7 5.5 %collective-permute-start.11 = (bf16[272,128]{1,0:T(8,128)(2,1)S(1)}, bf16[272,128]{1,0:T(8,128)(2,1)S(1)}, u32[]{:S(2)}, u32[]{:S(2)}) collective-permute-start(bf16[272,128]{1,0:T(8,128)(2,1)S(1)} %get-tuple-element.29), channel_id=1, source_target_pairs={{0,1},{1,0},{2,3},{3,2},{4,5},{5,4},{6,7},{7,6},{8,9},{9,8},{10,11... | collective-permute-start | bytes 208904 | tf_op jit(solution)/shard_map/ppermute | solution.py:430
  31.2 0.1 pad_add_fusion.place_ref.refs_0_
  31.3 2.8 %collective-permute-done.11.ask.refs_1_ = bf16[272,128]{1,0:T(8,128)(2,1)S(1)} collective-permute-done((bf16[272,128]{1,0:T(8,128)(2,1)S(1)}, bf16[272,128]{1,0:T(8,128)(2,1)S(1)}, u32[]{:S(2)}, u32[]{:S(2)}) %collective-permute-start.11) | collective-permute-done | bytes 69664 | tf_op jit(solution)/shard_map/ppermute | solution.py:430
  34.1 0.0 copy-done.4
  34.1 0.8 count.1
  35.0 5.4 %collective-permute-done.9.refs_2_.refs_6_ = bf16[384,256]{1,0:T(8,128)(2,1)S(1)} collective-permute-done((bf16[384,256]{1,0:T(8,128)(2,1)S(1)}, bf16[384,256]{1,0:T(8,128)(2,1)S(1)}, u32[]{:S(2)}, u32[]{:S(2)}) %collective-permute-start.9) | collective-permute-done | bytes 196640 | tf_op jit(solution)/shard_map/ppermute | solution.py:426
  40.4 0.6 collective-permute-start.10
  41.0 0.0 collective-permute-done.7.refs_1_.refs_5_
  41.0 1.6 %collective-permute-start.8 = (bf16[384,128]{1,0:T(8,128)(2,1)S(1)}, bf16[384,128]{1,0:T(8,128)(2,1)S(1)}, u32[]{:S(2)}, u32[]{:S(2)}) collective-permute-start(bf16[384,128]{1,0:T(8,128)(2,1)S(1)} %slice.18), channel_id=1, source_target_pairs={{0,16},{16,32},{32,48},{48,0},{1,17},{17,33},{33,49},{49,1},{2,18}... | collective-permute-start | bytes 294920 | tf_op jit(solution)/shard_map/ppermute | solution.py:426
  42.6 0.0 copy-start.6
  42.6 1.1 copy-done.6
  43.7 6.4 %shard_map.112 = (f32[8,384,128]{2,1,0:T(8,128)S(1)}, f32[8,384,128]{2,1,0:T(8,128)S(1)}, f32[8,384,128]{2,1,0:T(8,128)S(1)}) custom-call(s32[2]{0:T(128)S(1)} %pad_add_fusion.place_ref.refs_0_, bf16[384,1024]{1,0:T(8,128)(2,1)S(1)} %bitcast.19, bf16[384,256]{1,0:T(8,128)(2,1)S(1)} %pad_maximum_fusion.1.refs_0_.refs_4_, ...), custom_call_target="tpu_custom_call" | custom-call | flops 1811939328 | bytes 1048576 | tf_op jit(solution)/shard_map/pallas_call | solution.py:251
  50.2 0.0 collective-permute-done.3.refs_0_.refs_10_
  50.2 0.1 slice.16
  50.2 1.3 %collective-permute-start.5 = (bf16[3,384,128]{2,1,0:T(8,128)(2,1)S(1)}, bf16[3,384,128]{2,1,0:T(8,128)(2,1)S(1)}, u32[]{:S(2)}, u32[]{:S(2)}) collective-permute-start(bf16[3,384,128]{2,1,0:T(8,128)(2,1)S(1)} %slice.16), channel_id=1, source_target_pairs={{0,16},{16,32},{32,48},{48,0},{1,17},{17,33},{33,49},{49,1},{2,18}... | collective-permute-start | bytes 884744 | tf_op jit(solution)/shard_map/ppermute | solution.py:426
  51.5 0.0 collective-permute-done.4.refs_1_.refs_11_
  51.5 0.1 slice.17
  51.6 1.1 collective-permute-start.6
  52.6 0.0 collective-permute-done.10.refs_2_.refs_8_
  52.6 0.0 collective-permute-done.8.refs_1_.refs_7_
  52.6 6.8 %shard_map.113 = (f32[8,384,128]{2,1,0:T(8,128)S(1)}, f32[8,384,128]{2,1,0:T(8,128)S(1)}, f32[8,384,128]{2,1,0:T(8,128)S(1)}) custom-call(s32[2]{0:T(128)S(1)} %pad_add_fusion.place_ref.refs_0_, bf16[384,1024]{1,0:T(8,128)(2,1)S(1)} %bitcast.20, bf16[3,384,256]{2,1,0:T(8,128)(2,1)S(1)} %pad_maximum_fusion.refs_0_.refs_9_, ...), custom_call_target="tpu_custom_call", output_to_operand_aliasing={{0}: (5, {})} | custom-call | flops 2415919104 | bytes 1048576 | tf_op jit(solution)/shard_map/pallas_call | solution.py:251
  59.5 7.2 %shard_map.114 = (f32[8,384,128]{2,1,0:T(8,128)S(1)}, f32[8,384,128]{2,1,0:T(8,128)S(1)}, f32[8,384,128]{2,1,0:T(8,128)S(1)}) custom-call(s32[2]{0:T(128)S(1)} %pad_add_fusion.place_ref.refs_0_, bf16[384,1024]{1,0:T(8,128)(2,1)S(1)} %bitcast.21, bf16[3,384,256]{2,1,0:T(8,128)(2,1)S(1)} %collective-permute-done.3.refs_0_.refs_10_, ...), custom_call_target="tpu_custom_call", output_to_operand_aliasing={{0}: (4, {})} | custom-call | flops 2415919104 | bytes 1048576 | tf_op jit(solution)/shard_map/pallas_call | solution.py:251
  66.6 0.0 collective-permute-done.5.refs_2_.refs_12_
  66.7 0.0 collective-permute-done.6.refs_3_.refs_13_
  66.7 4.8 %context.1 = bf16[400,128]{1,0:T(8,128)(2,1)S(1)} custom-call(s32[2]{0:T(128)S(1)} %pad_add_fusion.place_ref.refs_0_, bf16[272,128]{1,0:T(8,128)(2,1)S(1)} %collective-permute-done.11.ask.refs_1_, f32[16,32,384]{2,1,0:T(8,128)S(1)} %get-tuple-element.30.refs_2_, bf16[16,64,384]{2,1,0:T(8,128)(2,1)S(1)} %get-tuple-element.31.refs_3_, ...), custom_call_target="tpu_custom_call" | custom-call | flops 805306368 | bytes 4194304 | tf_op jit(solution)/shard_map/context/pallas_call | solution.py:372
  71.4 5.5 %collective-permute-start.12 = (bf16[400,128]{1,0:T(8,128)(2,1)S(1)}, bf16[400,128]{1,0:T(8,128)(2,1)S(1)}, u32[]{:S(2)}, u32[]{:S(2)}) collective-permute-start(bf16[400,128]{1,0:T(8,128)(2,1)S(1)} %context.1), channel_id=1, source_target_pairs={{0,1},{1,0},{2,3},{3,2},{4,5},{5,4},{6,7},{7,6},{8,9},{9,8},{10,11... | collective-permute-start | bytes 307208 | tf_op jit(solution)/shard_map/ppermute | solution.py:430
  76.9 44.9 %shard_map.115 = bf16[384,1024]{1,0:T(8,128)(2,1)} custom-call(s32[2]{0:T(128)S(1)} %pad_add_fusion.place_ref.refs_0_, bf16[384,1024]{1,0:T(8,128)(2,1)S(1)} %bitcast.22, bf16[3,384,256]{2,1,0:T(8,128)(2,1)S(1)} %collective-permute-done.3.refs_0_.refs_10_, bf16[3,384,256]{2,1,0:T(8,128)(2,1)S(1)} %collective-permute-done.4.refs_1_.refs_11_, ...), custom_call_target="tpu_custom_call" | custom-call | flops 3019898880 | bytes 1048576 | tf_op jit(solution)/shard_map/pallas_call | solution.py:251
  121.8 0.0 collective-permute-done.12.back
  121.8 0.9 finish.1
  (2 shorter events, 0.0 us)
Async XLA Ops:
  0.6 24.2 %copy-start.3 = (s32[1,8,16]{2,1,0:T(8,128)S(1)}, s32[1,8,16]{2,1,0:T(8,128)}, u32[]{:S(2)}) copy-start(s32[1,8,16]{2,1,0:T(8,128)} %param.15) | copy-start | bytes 1540
  0.6 24.2 %copy-start.1 = (bf16[1,8,4,128]{3,2,1,0:T(4,128)(2,1)S(1)}, bf16[1,8,4,128]{3,2,1,0:T(4,128)(2,1)}, u32[]{:S(2)}) copy-start(bf16[1,8,4,128]{3,2,1,0:T(4,128)(2,1)} %param.13) | copy-start | bytes 24580
  0.7 24.2 %copy-start.2 = (bf16[1,8,4,128]{3,2,1,0:T(4,128)(2,1)S(1)}, bf16[1,8,4,128]{3,2,1,0:T(4,128)(2,1)}, u32[]{:S(2)}) copy-start(bf16[1,8,4,128]{3,2,1,0:T(4,128)(2,1)} %param.14) | copy-start | bytes 24580
  0.7 24.2 %copy-start = (bf16[1,8,4,1024]{3,2,1,0:T(4,128)(2,1)S(1)}, bf16[1,8,4,1024]{3,2,1,0:T(4,128)(2,1)}, u32[]{:S(2)}) copy-start(bf16[1,8,4,1024]{3,2,1,0:T(4,128)(2,1)} %param.12) | copy-start | bytes 196612
  0.7 24.2 %copy-start.5 = (s32[1,8]{1,0:T(1,128)S(1)}, s32[1,8]{1,0:T(1,128)}, u32[]{:S(2)}) copy-start(s32[1,8]{1,0:T(1,128)} %length.1) | copy-start | bytes 100
  0.7 33.4 %copy-start.4 = (bf16[8,128]{1,0:T(8,128)(2,1)S(1)}, bf16[8,128]{1,0:T(8,128)(2,1)}, u32[]{:S(2)}) copy-start(bf16[8,128]{1,0:T(8,128)(2,1)} %check.1) | copy-start | bytes 6148
  1.7 7.1 %collective-permute-start = (bf16[384,256]{1,0:T(8,128)(2,1)S(1)}, bf16[384,256]{1,0:T(8,128)(2,1)S(1)}, u32[]{:S(2)}, u32[]{:S(2)}) collective-permute-start(bf16[384,256]{1,0:T(8,128)(2,1)S(1)} %pad_maximum_fusion.1.refs_0_.refs_4_), channel_id=1, source_target_pairs={{0,64},{64,128},{128,192},{192,0},{1,65},{65,129},{129,193},{193,1... | collective-permute-start | bytes 589832 | tf_op jit(solution)/shard_map/ppermute | solution.py:426
  1.8 18.8 %collective-permute-start.1 = (bf16[384,256]{1,0:T(8,128)(2,1)S(1)}, bf16[384,256]{1,0:T(8,128)(2,1)S(1)}, u32[]{:S(2)}, u32[]{:S(2)}) collective-permute-start(bf16[384,256]{1,0:T(8,128)(2,1)S(1)} %pad_maximum_fusion.1.refs_0_.refs_4_), channel_id=1, source_target_pairs={{0,128},{64,192},{128,0},{192,64},{1,129},{65,193},{129,1},{193,65... | collective-permute-start | bytes 589832 | tf_op jit(solution)/shard_map/ppermute | solution.py:426
  3.4 17.3 %collective-permute-start.2 = (bf16[384,256]{1,0:T(8,128)(2,1)S(1)}, bf16[384,256]{1,0:T(8,128)(2,1)S(1)}, u32[]{:S(2)}, u32[]{:S(2)}) collective-permute-start(bf16[384,256]{1,0:T(8,128)(2,1)S(1)} %pad_maximum_fusion.1.refs_0_.refs_4_), channel_id=1, source_target_pairs={{0,192},{64,0},{128,64},{192,128},{1,193},{65,1},{129,65},{193,129... | collective-permute-start | bytes 589832 | tf_op jit(solution)/shard_map/ppermute | solution.py:426
  20.7 29.5 %collective-permute-start.3 = (bf16[3,384,256]{2,1,0:T(8,128)(2,1)S(1)}, bf16[3,384,256]{2,1,0:T(8,128)(2,1)S(1)}, u32[]{:S(2)}, u32[]{:S(2)}) collective-permute-start(bf16[3,384,256]{2,1,0:T(8,128)(2,1)S(1)} %pad_maximum_fusion.refs_0_.refs_9_), channel_id=1, source_target_pairs={{0,16},{16,32},{32,48},{48,0},{1,17},{17,33},{33,49},{49,1},{2,18}... | collective-permute-start | bytes 1769480 | tf_op jit(solution)/shard_map/ppermute | solution.py:426
  22.3 29.2 %collective-permute-start.4 = (bf16[3,384,256]{2,1,0:T(8,128)(2,1)S(1)}, bf16[3,384,256]{2,1,0:T(8,128)(2,1)S(1)}, u32[]{:S(2)}, u32[]{:S(2)}) collective-permute-start(bf16[3,384,256]{2,1,0:T(8,128)(2,1)S(1)} %pad_maximum_fusion.refs_0_.refs_9_), channel_id=1, source_target_pairs={{0,48},{16,0},{32,16},{48,32},{1,49},{17,1},{33,17},{49,33},{2,50}... | collective-permute-start | bytes 1769480 | tf_op jit(solution)/shard_map/ppermute | solution.py:426
  22.8 17.6 %collective-permute-start.9 = (bf16[384,256]{1,0:T(8,128)(2,1)S(1)}, bf16[384,256]{1,0:T(8,128)(2,1)S(1)}, u32[]{:S(2)}, u32[]{:S(2)}) collective-permute-start(bf16[384,256]{1,0:T(8,128)(2,1)S(1)} %pad_maximum_fusion.1.refs_0_.refs_4_), channel_id=1, source_target_pairs={{0,48},{16,0},{32,16},{48,32},{1,49},{17,1},{33,17},{49,33},{2,50}... | collective-permute-start | bytes 589832 | tf_op jit(solution)/shard_map/ppermute | solution.py:426
  24.5 16.5 %collective-permute-start.7 = (bf16[384,256]{1,0:T(8,128)(2,1)S(1)}, bf16[384,256]{1,0:T(8,128)(2,1)S(1)}, u32[]{:S(2)}, u32[]{:S(2)}) collective-permute-start(bf16[384,256]{1,0:T(8,128)(2,1)S(1)} %pad_maximum_fusion.1.refs_0_.refs_4_), channel_id=1, source_target_pairs={{0,16},{16,32},{32,48},{48,0},{1,17},{17,33},{33,49},{49,1},{2,18}... | collective-permute-start | bytes 589832 | tf_op jit(solution)/shard_map/ppermute | solution.py:426
  25.7 8.4 %collective-permute-start.11 = (bf16[272,128]{1,0:T(8,128)(2,1)S(1)}, bf16[272,128]{1,0:T(8,128)(2,1)S(1)}, u32[]{:S(2)}, u32[]{:S(2)}) collective-permute-start(bf16[272,128]{1,0:T(8,128)(2,1)S(1)} %get-tuple-element.29), channel_id=1, source_target_pairs={{0,1},{1,0},{2,3},{3,2},{4,5},{5,4},{6,7},{7,6},{8,9},{9,8},{10,11... | collective-permute-start | bytes 208904 | tf_op jit(solution)/shard_map/ppermute | solution.py:430
  40.4 12.2 %collective-permute-start.10 = (bf16[384,128]{1,0:T(8,128)(2,1)S(1)}, bf16[384,128]{1,0:T(8,128)(2,1)S(1)}, u32[]{:S(2)}, u32[]{:S(2)}) collective-permute-start(bf16[384,128]{1,0:T(8,128)(2,1)S(1)} %slice.19), channel_id=1, source_target_pairs={{0,48},{16,0},{32,16},{48,32},{1,49},{17,1},{33,17},{49,33},{2,50}... | collective-permute-start | bytes 294920 | tf_op jit(solution)/shard_map/ppermute | solution.py:426
  41.0 11.6 %collective-permute-start.8 = (bf16[384,128]{1,0:T(8,128)(2,1)S(1)}, bf16[384,128]{1,0:T(8,128)(2,1)S(1)}, u32[]{:S(2)}, u32[]{:S(2)}) collective-permute-start(bf16[384,128]{1,0:T(8,128)(2,1)S(1)} %slice.18), channel_id=1, source_target_pairs={{0,16},{16,32},{32,48},{48,0},{1,17},{17,33},{33,49},{49,1},{2,18}... | collective-permute-start | bytes 294920 | tf_op jit(solution)/shard_map/ppermute | solution.py:426
  42.6 1.1 copy-start.6
  50.2 16.4 %collective-permute-start.5 = (bf16[3,384,128]{2,1,0:T(8,128)(2,1)S(1)}, bf16[3,384,128]{2,1,0:T(8,128)(2,1)S(1)}, u32[]{:S(2)}, u32[]{:S(2)}) collective-permute-start(bf16[3,384,128]{2,1,0:T(8,128)(2,1)S(1)} %slice.16), channel_id=1, source_target_pairs={{0,16},{16,32},{32,48},{48,0},{1,17},{17,33},{33,49},{49,1},{2,18}... | collective-permute-start | bytes 884744 | tf_op jit(solution)/shard_map/ppermute | solution.py:426
  51.6 15.1 %collective-permute-start.6 = (bf16[3,384,128]{2,1,0:T(8,128)(2,1)S(1)}, bf16[3,384,128]{2,1,0:T(8,128)(2,1)S(1)}, u32[]{:S(2)}, u32[]{:S(2)}) collective-permute-start(bf16[3,384,128]{2,1,0:T(8,128)(2,1)S(1)} %slice.17), channel_id=1, source_target_pairs={{0,48},{16,0},{32,16},{48,32},{1,49},{17,1},{33,17},{49,33},{2,50}... | collective-permute-start | bytes 884744 | tf_op jit(solution)/shard_map/ppermute | solution.py:426
  71.4 50.4 %collective-permute-start.12 = (bf16[400,128]{1,0:T(8,128)(2,1)S(1)}, bf16[400,128]{1,0:T(8,128)(2,1)S(1)}, u32[]{:S(2)}, u32[]{:S(2)}) collective-permute-start(bf16[400,128]{1,0:T(8,128)(2,1)S(1)} %context.1), channel_id=1, source_target_pairs={{0,1},{1,0},{2,3},{3,2},{4,5},{5,4},{6,7},{7,6},{8,9},{9,8},{10,11... | collective-permute-start | bytes 307208 | tf_op jit(solution)/shard_map/ppermute | solution.py:430

commit v2 on v1

--- a/solution.py
+++ b/solution.py
@@ -127,9 +127,9 @@
 def fold_moving(before, after, h, q, blocks):
     m_ref, l_ref, a_ref = after
 
-    @pl.loop(0, ROWS // HD)
+    @pl.loop(0, ROWS // 32)
     def _(i):
-        rows = pl.ds(pl.multiple_of(i * HD, HD), HD)
+        rows = pl.ds(pl.multiple_of(i * 32, 32), 32)
         l_ref[h, rows] = before[1][h, rows]
         a_ref[h, rows] = before[2][h, rows]
         for b in blocks:
@@ -187,52 +187,46 @@
             lanes = pl.ds(pl.multiple_of(h * HD, HD), HD)
             return lambda rows=slice(None): q_ref[rows, lanes]
 
+        def close(h):
+            share = 1.0 / jnp.sum(after[1][h], axis=1, keepdims=True)
+            out[:, pl.ds(pl.multiple_of(h * HD, HD), HD)] = (after[2][h] * share).astype(bf16)
+
+        source = after if own is not None else before
+
+        def rest(z, x):
+            held = None
+            for holds, _, _ in cases:
+                held = holds(z, x) if held is None else held | holds(z, x)
+            return jnp.logical_not(held)
+
         def run(folded, slow):
-            if own is not None:
-
-                @pl.loop(0, HEADS // PAIR)
-                def _(i):
-                    for n in range(PAIR):
-                        h = i * PAIR + n
-                        fold_own(after, h, query_of(h), own(blocks))
-
-            source = after if own is not None else before
-            idle = None
-            for holds, step, some in cases:
-                held = holds(z, x)
-                idle = held if idle is None else idle | held
+            for holds, step, some in cases + [(rest, 1, [])]:
                 if slow:
                     step = 1
 
-                @pl.when(held)
+                @pl.when(holds(z, x))
                 def _(some=some, step=step):
                     @pl.loop(0, HEADS // step)
                     def _(i):
-                        for n in range(step):
-                            h = i * step + n
-                            folded(source, after, h, query_of(h), some)
-
-            if own is None:
-
-                @pl.when(jnp.logical_not(idle))
-                def _():
-                    @pl.loop(0, HEADS)
-                    def _(h):
-                        after[1][h] = before[1][h]
-                        after[2][h] = before[2][h]
+                        heads = [i * step + n for n in range(step)]
+                        if own is not None:
+                            for h in heads:
+                                fold_own(after, h, query_of(h), own(blocks))
+                        for h in heads:
+                            if some:
+                                folded(source, after, h, query_of(h), some)
+                            elif own is None:
+                                after[1][h] = before[1][h]
+                                after[2][h] = before[2][h]
+                        if last:
+                            for h in heads:
+                                close(h)
 
         run(fold_fixed, False)
 
         @pl.when(too_large(after[1]))
         def _():
             run(fold_moving, True)
-
-        if last:
-
-            @pl.loop(0, HEADS)
-            def _(h):
-                total = jnp.sum(after[1][h], axis=1, keepdims=True)
-                out[:, pl.ds(pl.multiple_of(h * HD, HD), HD)] = (after[2][h] / total).astype(bf16)
 
     vmem = pl.BlockSpec(memory_space=pltpu.VMEM)
     shape = jax.ShapeDtypeStruct(STATE, f32)
@@ -303,27 +297,23 @@
     def index(dz, dx):
         return ((z + 4 - dz) % 4) * 4 + (x + 4 - dx) % 4
 
-    def apply(dz, dx, block):
-        b = index(dz, dx)
-        scores = dot_t(q, block.key()) * SCALE
-        each = jnp.concatenate([each_ref[b]] * HEADS, axis=0)
-        return b, scores, each
-
     level = jnp.max(dot_t(q, held[0][2].key()), axis=1, keepdims=True) * SCALE
     level = jnp.maximum(jnp.full((QROWS, HD), LOW), level)
     total = jnp.zeros((QROWS, HD), f32)
     mixed = jnp.zeros((QROWS + REQ * CSW, HD), f32)
     digest_k = jnp.zeros((REQ * CSW, HD), f32)
-    for dz, dx, block in held:
-        b, scores, each = apply(dz, dx, block)
-        weights = [
-            jnp.exp2(scores[:, i : i + HD] - level) * each[:, i : i + HD] for i in range(0, ROWS, HD)
-        ]
-        total = total + (weights[0] + weights[1] + weights[2])
-        weighted = weighted_ref[b]
-        left = jnp.concatenate([jnp.concatenate([w.astype(bf16) for w in weights], axis=1), weighted], axis=0)
-        mixed = mixed + dot(left, block.value())
-        digest_k = digest_k + dot(weighted, block.key())
+    places = [(index(dz, dx), slice(i, i + HD)) for dz, dx, _ in held for i in range(0, ROWS, HD)]
+    for c, (k, v) in enumerate(chunks_of([block for _, _, block in held])):
+        scores = dot_t(q, k) * SCALE
+        weights = []
+        for n, (b, lanes) in enumerate(places[2 * c : 2 * c + 2]):
+            each = jnp.concatenate([each_ref[b, :, lanes]] * HEADS, axis=0)
+            w = jnp.exp2(scores[:, n * HD : (n + 1) * HD] - level) * each
+            total = total + w
+            weights.append(w.astype(bf16))
+        weighted = jnp.concatenate([weighted_ref[b, :, lanes] for b, lanes in places[2 * c : 2 * c + 2]], axis=1)
+        mixed = mixed + dot(jnp.concatenate([jnp.concatenate(weights, axis=1), weighted], axis=0), v)
+        digest_k = digest_k + dot(weighted, k)
     m_ref[...] = level
     l_ref[...] = jnp.broadcast_to(jnp.sum(total, axis=1, keepdims=True), (QROWS, HD))
     a_ref[...] = mixed
@@ -459,7 +449,7 @@
     state = part(
         lambda r: [
             (lambda z, x: x == 3, PAIR, [both(r[1]), both(r[2])]),
-            (lambda z, x: (x >= 1) & (x < 3), PAIR, [both(r[1])]),
+            (lambda z, x: (x >= 1) & (x < 3), 1, [both(r[1])]),
         ],
         place,
         query,
@@ -478,8 +468,8 @@
         ups = [both(r[0], n) for n in range(3)]
         far = [Block(r[1], 0, r[2], 0)]
         return [
-            (lambda z, x: (z == 3) & (x >= 2), PAIR, ups + far),
-            (lambda z, x: (z == 3) & (x < 2), 1, ups),
+            (lambda z, x: (z == 3) & (x >= 2), 4, ups + far),
+            (lambda z, x: (z == 3) & (x < 2), 4, ups),
             (lambda z, x: (z == 2) & (x >= 2), 1, ups[:2] + far),
             (lambda z, x: (z == 2) & (x < 2), 1, ups[:2]),
             (lambda z, x: (z == 1) & (x >= 2), 1, ups[:1] + far),
@@ -495,7 +485,10 @@
         return [both(r[0], n), both(r[1], n)]
 
     state = part(
-        lambda r: [(lambda z, x: z >= 2, PAIR, beside(r, 0) + beside(r, 1)), (lambda z, x: z == 1, 1, beside(r, 0))],
+        lambda r: [
+            (lambda z, x: z >= 2, 4, beside(r, 0) + beside(r, 1)),
+            (lambda z, x: z == 1, 1, beside(r, 0)),
+        ],
         place,
         query,
         [up_right, up_left],
@@ -527,8 +520,8 @@
     def rest(r):
         far = [Block(r[2], 0, r[3], 0, n) for n in range(3)]
         return [
-            (lambda z, x: z == 3, PAIR, beside(r, 2) + far),
-            (lambda z, x: z == 2, 1, far[:2]),
+            (lambda z, x: z == 3, 4, beside(r, 2) + far),
+            (lambda z, x: z == 2, PAIR, far[:2]),
             (lambda z, x: z == 1, 1, far[:1]),
         ]
 

time: 123 us -> 212 us (1.72)
  Pallas kernels: 72.7 us -> 162 us
    pallas_call x4, Pallas kernels: 65.3 us -> 156 us  [part(): pl.pallas_call(body, in_specs=[smem()] + [vmem] * (1 + count + len(carrie...]
  transfers between devices with their start and end apart: 13 -> 13, of which waited for: 4 -> 4; matrix products, arithmetic and copies ran while one was open for 0% -> 0% of each run, Pallas kernels for 55% -> 74%
where the time goes in v2:
time: 212 us
  Pallas kernels  162 us (76%)
  waiting for transfers between devices  25.1 us (12%)
  starting transfers between devices  21.7 us (10%)
    pallas_call x4, Pallas kernels, part(): pl.pallas_call(body, in_specs=[smem()] + [vmem] * (1 + count + len(carrie...  156 us
    ppermute x11, waiting for transfers between devices, turn(): return lax.ppermute(shard, axis, [(i, (i + by) % n) for i in range(n)])  22.3 us
    ppermute x2, starting transfers between devices, swap(): return lax.ppermute(shard, 'grp', [(0, 1), (1, 0)])  11 us
    ppermute x11, starting transfers between devices, turn(): return lax.ppermute(shard, axis, [(i, (i + by) % n) for i in range(n)])  10.8 us
  transfers between devices with their start and end apart: 13, of which 4 were waited for; matrix products, arithmetic and copies ran while one was open for 0% of the time, Pallas kernels for 74%

profile of v2, /device:TPU:114, one launch (start us, length us, event | category | flops | bytes accessed | tf_op | source)
XLA Modules:
  0.0 212.1 jit_solution(5193591395013981130)
XLA Ops:
  0.6 0.0 copy-start.3
  0.6 0.0 copy-start.1
  0.7 0.0 copy-start.2
  0.7 0.0 copy-start
  0.7 0.0 copy-start.5
  0.7 0.0 copy-start.4
  0.7 1.0 pad_maximum_fusion.1.refs_0_.refs_4_
  1.7 0.1 collective-permute-start
  1.8 1.6 collective-permute-start.1
  3.4 0.5 collective-permute-start.2
  3.8 5.0 %collective-permute-done = bf16[384,256]{1,0:T(8,128)(2,1)S(1)} collective-permute-done((bf16[384,256]{1,0:T(8,128)(2,1)S(1)}, bf16[384,256]{1,0:T(8,128)(2,1)S(1)}, u32[]{:S(2)}, u32[]{:S(2)}) %collective-permute-start) | collective-permute-done | bytes 196640 | tf_op jit(solution)/shard_map/ppermute | solution.py:416
  8.8 11.8 %collective-permute-done.1 = bf16[384,256]{1,0:T(8,128)(2,1)S(1)} collective-permute-done((bf16[384,256]{1,0:T(8,128)(2,1)S(1)}, bf16[384,256]{1,0:T(8,128)(2,1)S(1)}, u32[]{:S(2)}, u32[]{:S(2)}) %collective-permute-start.1) | collective-permute-done | bytes 196640 | tf_op jit(solution)/shard_map/ppermute | solution.py:416
  20.6 0.0 collective-permute-done.2
  20.6 0.1 pad_maximum_fusion.refs_0_.refs_9_
  20.7 1.6 collective-permute-start.3
  22.3 0.5 collective-permute-start.4
  22.8 1.7 collective-permute-start.9
  24.5 0.3 collective-permute-start.7
  24.8 0.0 copy-done.3
  24.8 0.0 copy-done.1
  24.8 0.0 copy-done.2
  24.8 0.0 copy-done
  24.8 0.0 copy-done.5
  24.8 0.9 prepare.1
  25.7 5.5 %collective-permute-start.11 = (bf16[272,128]{1,0:T(8,128)(2,1)S(1)}, bf16[272,128]{1,0:T(8,128)(2,1)S(1)}, u32[]{:S(2)}, u32[]{:S(2)}) collective-permute-start(bf16[272,128]{1,0:T(8,128)(2,1)S(1)} %get-tuple-element.29), channel_id=1, source_target_pairs={{0,1},{1,0},{2,3},{3,2},{4,5},{5,4},{6,7},{7,6},{8,9},{9,8},{10,11... | collective-permute-start | bytes 208904 | tf_op jit(solution)/shard_map/ppermute | solution.py:420
  31.2 0.1 pad_add_fusion.place_ref.refs_0_
  31.3 2.8 %collective-permute-done.11.ask.refs_1_ = bf16[272,128]{1,0:T(8,128)(2,1)S(1)} collective-permute-done((bf16[272,128]{1,0:T(8,128)(2,1)S(1)}, bf16[272,128]{1,0:T(8,128)(2,1)S(1)}, u32[]{:S(2)}, u32[]{:S(2)}) %collective-permute-start.11) | collective-permute-done | bytes 69664 | tf_op jit(solution)/shard_map/ppermute | solution.py:420
  34.1 0.0 copy-done.4
  34.1 0.8 count.1
  35.0 5.4 %collective-permute-done.9.refs_2_.refs_6_ = bf16[384,256]{1,0:T(8,128)(2,1)S(1)} collective-permute-done((bf16[384,256]{1,0:T(8,128)(2,1)S(1)}, bf16[384,256]{1,0:T(8,128)(2,1)S(1)}, u32[]{:S(2)}, u32[]{:S(2)}) %collective-permute-start.9) | collective-permute-done | bytes 196640 | tf_op jit(solution)/shard_map/ppermute | solution.py:416
  40.4 0.6 collective-permute-start.10
  41.0 0.0 collective-permute-done.7.refs_1_.refs_5_
  41.0 1.6 collective-permute-start.8
  42.6 0.0 copy-start.6
  42.6 1.1 copy-done.6
  43.7 7.0 %shard_map.112 = (f32[8,384,128]{2,1,0:T(8,128)S(1)}, f32[8,384,128]{2,1,0:T(8,128)S(1)}, f32[8,384,128]{2,1,0:T(8,128)S(1)}) custom-call(s32[2]{0:T(128)S(1)} %pad_add_fusion.place_ref.refs_0_, bf16[384,1024]{1,0:T(8,128)(2,1)S(1)} %bitcast.19, bf16[384,256]{1,0:T(8,128)(2,1)S(1)} %pad_maximum_fusion.1.refs_0_.refs_4_, ...), custom_call_target="tpu_custom_call" | custom-call | flops 1811939328 | bytes 1048576 | tf_op jit(solution)/shard_map/pallas_call | solution.py:245
  50.7 0.0 collective-permute-done.3.refs_0_.refs_10_
  50.7 0.1 slice.16
  50.8 1.5 collective-permute-start.5
  52.2 0.0 collective-permute-done.4.refs_1_.refs_11_
  52.3 0.1 slice.17
  52.3 0.9 collective-permute-start.6
  53.2 0.0 collective-permute-done.10.refs_2_.refs_8_
  53.2 0.0 collective-permute-done.8.refs_1_.refs_7_
  53.2 5.2 %shard_map.113 = (f32[8,384,128]{2,1,0:T(8,128)S(1)}, f32[8,384,128]{2,1,0:T(8,128)S(1)}, f32[8,384,128]{2,1,0:T(8,128)S(1)}) custom-call(s32[2]{0:T(128)S(1)} %pad_add_fusion.place_ref.refs_0_, bf16[384,1024]{1,0:T(8,128)(2,1)S(1)} %bitcast.20, bf16[3,384,256]{2,1,0:T(8,128)(2,1)S(1)} %pad_maximum_fusion.refs_0_.refs_9_, ...), custom_call_target="tpu_custom_call", output_to_operand_aliasing={{0}: (5, {})} | custom-call | flops 2415919104 | bytes 1048576 | tf_op jit(solution)/shard_map/pallas_call | solution.py:245
  58.4 6.6 %shard_map.114 = (f32[8,384,128]{2,1,0:T(8,128)S(1)}, f32[8,384,128]{2,1,0:T(8,128)S(1)}, f32[8,384,128]{2,1,0:T(8,128)S(1)}) custom-call(s32[2]{0:T(128)S(1)} %pad_add_fusion.place_ref.refs_0_, bf16[384,1024]{1,0:T(8,128)(2,1)S(1)} %bitcast.21, bf16[3,384,256]{2,1,0:T(8,128)(2,1)S(1)} %collective-permute-done.3.refs_0_.refs_10_, ...), custom_call_target="tpu_custom_call", output_to_operand_aliasing={{0}: (4, {})} | custom-call | flops 2415919104 | bytes 1048576 | tf_op jit(solution)/shard_map/pallas_call | solution.py:245
  65.0 0.0 collective-permute-done.5.refs_2_.refs_12_
  65.0 0.0 collective-permute-done.6.refs_3_.refs_13_
  65.0 3.6 %context.1 = bf16[400,128]{1,0:T(8,128)(2,1)S(1)} custom-call(s32[2]{0:T(128)S(1)} %pad_add_fusion.place_ref.refs_0_, bf16[272,128]{1,0:T(8,128)(2,1)S(1)} %collective-permute-done.11.ask.refs_1_, f32[16,32,384]{2,1,0:T(8,128)S(1)} %get-tuple-element.30.refs_2_, bf16[16,64,384]{2,1,0:T(8,128)(2,1)S(1)} %get-tuple-element.31.refs_3_, ...), custom_call_target="tpu_custom_call" | custom-call | flops 805306368 | bytes 4194304 | tf_op jit(solution)/shard_map/context/pallas_call | solution.py:362
  68.7 5.5 %collective-permute-start.12 = (bf16[400,128]{1,0:T(8,128)(2,1)S(1)}, bf16[400,128]{1,0:T(8,128)(2,1)S(1)}, u32[]{:S(2)}, u32[]{:S(2)}) collective-permute-start(bf16[400,128]{1,0:T(8,128)(2,1)S(1)} %context.1), channel_id=1, source_target_pairs={{0,1},{1,0},{2,3},{3,2},{4,5},{5,4},{6,7},{7,6},{8,9},{9,8},{10,11... | collective-permute-start | bytes 307208 | tf_op jit(solution)/shard_map/ppermute | solution.py:420
  74.2 137.1 %shard_map.115 = bf16[384,1024]{1,0:T(8,128)(2,1)} custom-call(s32[2]{0:T(128)S(1)} %pad_add_fusion.place_ref.refs_0_, bf16[384,1024]{1,0:T(8,128)(2,1)S(1)} %bitcast.22, bf16[3,384,256]{2,1,0:T(8,128)(2,1)S(1)} %collective-permute-done.3.refs_0_.refs_10_, bf16[3,384,256]{2,1,0:T(8,128)(2,1)S(1)} %collective-permute-done.4.refs_1_.refs_11_, ...), custom_call_target="tpu_custom_call" | custom-call | flops 3019898880 | bytes 1048576 | tf_op jit(solution)/shard_map/pallas_call | solution.py:245
  211.2 0.0 collective-permute-done.12.back
  211.2 0.9 finish.1
  (2 shorter events, 0.0 us)
Async XLA Ops:
  0.6 24.2 %copy-start.3 = (s32[1,8,16]{2,1,0:T(8,128)S(1)}, s32[1,8,16]{2,1,0:T(8,128)}, u32[]{:S(2)}) copy-start(s32[1,8,16]{2,1,0:T(8,128)} %param.15) | copy-start | bytes 1540
  0.6 24.2 %copy-start.1 = (bf16[1,8,4,128]{3,2,1,0:T(4,128)(2,1)S(1)}, bf16[1,8,4,128]{3,2,1,0:T(4,128)(2,1)}, u32[]{:S(2)}) copy-start(bf16[1,8,4,128]{3,2,1,0:T(4,128)(2,1)} %param.13) | copy-start | bytes 24580
  0.7 24.2 %copy-start.2 = (bf16[1,8,4,128]{3,2,1,0:T(4,128)(2,1)S(1)}, bf16[1,8,4,128]{3,2,1,0:T(4,128)(2,1)}, u32[]{:S(2)}) copy-start(bf16[1,8,4,128]{3,2,1,0:T(4,128)(2,1)} %param.14) | copy-start | bytes 24580
  0.7 24.2 %copy-start = (bf16[1,8,4,1024]{3,2,1,0:T(4,128)(2,1)S(1)}, bf16[1,8,4,1024]{3,2,1,0:T(4,128)(2,1)}, u32[]{:S(2)}) copy-start(bf16[1,8,4,1024]{3,2,1,0:T(4,128)(2,1)} %param.12) | copy-start | bytes 196612
  0.7 24.2 %copy-start.5 = (s32[1,8]{1,0:T(1,128)S(1)}, s32[1,8]{1,0:T(1,128)}, u32[]{:S(2)}) copy-start(s32[1,8]{1,0:T(1,128)} %length.1) | copy-start | bytes 100
  0.7 33.4 %copy-start.4 = (bf16[8,128]{1,0:T(8,128)(2,1)S(1)}, bf16[8,128]{1,0:T(8,128)(2,1)}, u32[]{:S(2)}) copy-start(bf16[8,128]{1,0:T(8,128)(2,1)} %check.1) | copy-start | bytes 6148
  1.7 7.1 %collective-permute-start = (bf16[384,256]{1,0:T(8,128)(2,1)S(1)}, bf16[384,256]{1,0:T(8,128)(2,1)S(1)}, u32[]{:S(2)}, u32[]{:S(2)}) collective-permute-start(bf16[384,256]{1,0:T(8,128)(2,1)S(1)} %pad_maximum_fusion.1.refs_0_.refs_4_), channel_id=1, source_target_pairs={{0,64},{64,128},{128,192},{192,0},{1,65},{65,129},{129,193},{193,1... | collective-permute-start | bytes 589832 | tf_op jit(solution)/shard_map/ppermute | solution.py:416
  1.8 18.8 %collective-permute-start.1 = (bf16[384,256]{1,0:T(8,128)(2,1)S(1)}, bf16[384,256]{1,0:T(8,128)(2,1)S(1)}, u32[]{:S(2)}, u32[]{:S(2)}) collective-permute-start(bf16[384,256]{1,0:T(8,128)(2,1)S(1)} %pad_maximum_fusion.1.refs_0_.refs_4_), channel_id=1, source_target_pairs={{0,128},{64,192},{128,0},{192,64},{1,129},{65,193},{129,1},{193,65... | collective-permute-start | bytes 589832 | tf_op jit(solution)/shard_map/ppermute | solution.py:416
  3.4 17.3 %collective-permute-start.2 = (bf16[384,256]{1,0:T(8,128)(2,1)S(1)}, bf16[384,256]{1,0:T(8,128)(2,1)S(1)}, u32[]{:S(2)}, u32[]{:S(2)}) collective-permute-start(bf16[384,256]{1,0:T(8,128)(2,1)S(1)} %pad_maximum_fusion.1.refs_0_.refs_4_), channel_id=1, source_target_pairs={{0,192},{64,0},{128,64},{192,128},{1,193},{65,1},{129,65},{193,129... | collective-permute-start | bytes 589832 | tf_op jit(solution)/shard_map/ppermute | solution.py:416
  20.7 30.0 %collective-permute-start.3 = (bf16[3,384,256]{2,1,0:T(8,128)(2,1)S(1)}, bf16[3,384,256]{2,1,0:T(8,128)(2,1)S(1)}, u32[]{:S(2)}, u32[]{:S(2)}) collective-permute-start(bf16[3,384,256]{2,1,0:T(8,128)(2,1)S(1)} %pad_maximum_fusion.refs_0_.refs_9_), channel_id=1, source_target_pairs={{0,16},{16,32},{32,48},{48,0},{1,17},{17,33},{33,49},{49,1},{2,18}... | collective-permute-start | bytes 1769480 | tf_op jit(solution)/shard_map/ppermute | solution.py:416
  22.3 30.0 %collective-permute-start.4 = (bf16[3,384,256]{2,1,0:T(8,128)(2,1)S(1)}, bf16[3,384,256]{2,1,0:T(8,128)(2,1)S(1)}, u32[]{:S(2)}, u32[]{:S(2)}) collective-permute-start(bf16[3,384,256]{2,1,0:T(8,128)(2,1)S(1)} %pad_maximum_fusion.refs_0_.refs_9_), channel_id=1, source_target_pairs={{0,48},{16,0},{32,16},{48,32},{1,49},{17,1},{33,17},{49,33},{2,50}... | collective-permute-start | bytes 1769480 | tf_op jit(solution)/shard_map/ppermute | solution.py:416
  22.8 17.6 %collective-permute-start.9 = (bf16[384,256]{1,0:T(8,128)(2,1)S(1)}, bf16[384,256]{1,0:T(8,128)(2,1)S(1)}, u32[]{:S(2)}, u32[]{:S(2)}) collective-permute-start(bf16[384,256]{1,0:T(8,128)(2,1)S(1)} %pad_maximum_fusion.1.refs_0_.refs_4_), channel_id=1, source_target_pairs={{0,48},{16,0},{32,16},{48,32},{1,49},{17,1},{33,17},{49,33},{2,50}... | collective-permute-start | bytes 589832 | tf_op jit(solution)/shard_map/ppermute | solution.py:416
  24.5 16.5 %collective-permute-start.7 = (bf16[384,256]{1,0:T(8,128)(2,1)S(1)}, bf16[384,256]{1,0:T(8,128)(2,1)S(1)}, u32[]{:S(2)}, u32[]{:S(2)}) collective-permute-start(bf16[384,256]{1,0:T(8,128)(2,1)S(1)} %pad_maximum_fusion.1.refs_0_.refs_4_), channel_id=1, source_target_pairs={{0,16},{16,32},{32,48},{48,0},{1,17},{17,33},{33,49},{49,1},{2,18}... | collective-permute-start | bytes 589832 | tf_op jit(solution)/shard_map/ppermute | solution.py:416
  25.7 8.4 %collective-permute-start.11 = (bf16[272,128]{1,0:T(8,128)(2,1)S(1)}, bf16[272,128]{1,0:T(8,128)(2,1)S(1)}, u32[]{:S(2)}, u32[]{:S(2)}) collective-permute-start(bf16[272,128]{1,0:T(8,128)(2,1)S(1)} %get-tuple-element.29), channel_id=1, source_target_pairs={{0,1},{1,0},{2,3},{3,2},{4,5},{5,4},{6,7},{7,6},{8,9},{9,8},{10,11... | collective-permute-start | bytes 208904 | tf_op jit(solution)/shard_map/ppermute | solution.py:420
  40.4 12.8 %collective-permute-start.10 = (bf16[384,128]{1,0:T(8,128)(2,1)S(1)}, bf16[384,128]{1,0:T(8,128)(2,1)S(1)}, u32[]{:S(2)}, u32[]{:S(2)}) collective-permute-start(bf16[384,128]{1,0:T(8,128)(2,1)S(1)} %slice.19), channel_id=1, source_target_pairs={{0,48},{16,0},{32,16},{48,32},{1,49},{17,1},{33,17},{49,33},{2,50}... | collective-permute-start | bytes 294920 | tf_op jit(solution)/shard_map/ppermute | solution.py:416
  41.0 12.2 %collective-permute-start.8 = (bf16[384,128]{1,0:T(8,128)(2,1)S(1)}, bf16[384,128]{1,0:T(8,128)(2,1)S(1)}, u32[]{:S(2)}, u32[]{:S(2)}) collective-permute-start(bf16[384,128]{1,0:T(8,128)(2,1)S(1)} %slice.18), channel_id=1, source_target_pairs={{0,16},{16,32},{32,48},{48,0},{1,17},{17,33},{33,49},{49,1},{2,18}... | collective-permute-start | bytes 294920 | tf_op jit(solution)/shard_map/ppermute | solution.py:416
  42.6 1.1 copy-start.6
  50.8 14.2 %collective-permute-start.5 = (bf16[3,384,128]{2,1,0:T(8,128)(2,1)S(1)}, bf16[3,384,128]{2,1,0:T(8,128)(2,1)S(1)}, u32[]{:S(2)}, u32[]{:S(2)}) collective-permute-start(bf16[3,384,128]{2,1,0:T(8,128)(2,1)S(1)} %slice.16), channel_id=1, source_target_pairs={{0,16},{16,32},{32,48},{48,0},{1,17},{17,33},{33,49},{49,1},{2,18}... | collective-permute-start | bytes 884744 | tf_op jit(solution)/shard_map/ppermute | solution.py:416
  52.3 12.7 %collective-permute-start.6 = (bf16[3,384,128]{2,1,0:T(8,128)(2,1)S(1)}, bf16[3,384,128]{2,1,0:T(8,128)(2,1)S(1)}, u32[]{:S(2)}, u32[]{:S(2)}) collective-permute-start(bf16[3,384,128]{2,1,0:T(8,128)(2,1)S(1)} %slice.17), channel_id=1, source_target_pairs={{0,48},{16,0},{32,16},{48,32},{1,49},{17,1},{33,17},{49,33},{2,50}... | collective-permute-start | bytes 884744 | tf_op jit(solution)/shard_map/ppermute | solution.py:416
  68.7 142.6 %collective-permute-start.12 = (bf16[400,128]{1,0:T(8,128)(2,1)S(1)}, bf16[400,128]{1,0:T(8,128)(2,1)S(1)}, u32[]{:S(2)}, u32[]{:S(2)}) collective-permute-start(bf16[400,128]{1,0:T(8,128)(2,1)S(1)} %context.1), channel_id=1, source_target_pairs={{0,1},{1,0},{2,3},{3,2},{4,5},{5,4},{6,7},{7,6},{8,9},{9,8},{10,11... | collective-permute-start | bytes 307208 | tf_op jit(solution)/shard_map/ppermute | solution.py:420

commit v3 on v2

--- a/solution.py
+++ b/solution.py
@@ -466,34 +466,30 @@
 
     def rising(r):
         ups = [both(r[0], n) for n in range(3)]
-        far = [Block(r[1], 0, r[2], 0)]
         return [
-            (lambda z, x: (z == 3) & (x >= 2), 4, ups + far),
-            (lambda z, x: (z == 3) & (x < 2), 4, ups),
-            (lambda z, x: (z == 2) & (x >= 2), 1, ups[:2] + far),
-            (lambda z, x: (z == 2) & (x < 2), 1, ups[:2]),
-            (lambda z, x: (z == 1) & (x >= 2), 1, ups[:1] + far),
-            (lambda z, x: (z == 1) & (x < 2), 1, ups[:1]),
+            (lambda z, x: z == 3, 4, ups),
+            (lambda z, x: z == 2, PAIR, ups[:2]),
+            (lambda z, x: z == 1, PAIR, ups[:1]),
+        ]
+
+    state = part(rising, place, query, [up], state)
+    up_k = turn(up_right[:, :, :HD], "x", 1)
+    up_v = turn(up_left[:, :, HD:], "x", -1)
+
+    def beside(r, n):
+        return [both(r[0], n), both(r[1], n)]
+
+    def beside_far(r):
+        four, two, far = beside(r, 0) + beside(r, 1), beside(r, 0), [Block(r[2], 0, r[3], 0)]
+        return [
+            (lambda z, x: (z >= 2) & (x >= 2), 4, four + far),
+            (lambda z, x: (z >= 2) & (x < 2), 4, four),
+            (lambda z, x: (z == 1) & (x >= 2), 1, two + far),
+            (lambda z, x: (z == 1) & (x < 2), 1, two),
             (lambda z, x: (z == 0) & (x >= 2), 1, far),
         ]
 
-    state = part(rising, place, query, [up, far_k, far_v], state)
-    up_k = turn(up_right[:, :, :HD], "x", 1)
-    up_v = turn(up_left[:, :, HD:], "x", -1)
-
-    def beside(r, n):
-        return [both(r[0], n), both(r[1], n)]
-
-    state = part(
-        lambda r: [
-            (lambda z, x: z >= 2, 4, beside(r, 0) + beside(r, 1)),
-            (lambda z, x: z == 1, 1, beside(r, 0)),
-        ],
-        place,
-        query,
-        [up_right, up_left],
-        state,
-    )
+    state = part(beside_far, place, query, [up_right, up_left, far_k, far_v], state)
 
     def everything(r):
         own, right, left, far_k, far_v, up, up_right, up_left, up_k, up_v = r

time: 212 us -> 212 us (level)
  the two profiles are of different devices: /device:TPU:114 before, /device:TPU:106 now
where the time goes in v3:
time: 212 us
  Pallas kernels  162 us (76%)
  waiting for transfers between devices  25.1 us (12%)
  starting transfers between devices  21.7 us (10%)
    pallas_call x4, Pallas kernels, part(): pl.pallas_call(body, in_specs=[smem()] + [vmem] * (1 + count + len(carrie...  156 us
    ppermute x11, waiting for transfers between devices, turn(): return lax.ppermute(shard, axis, [(i, (i + by) % n) for i in range(n)])  22.3 us
    ppermute x2, starting transfers between devices, swap(): return lax.ppermute(shard, 'grp', [(0, 1), (1, 0)])  11 us
    ppermute x11, starting transfers between devices, turn(): return lax.ppermute(shard, axis, [(i, (i + by) % n) for i in range(n)])  10.8 us
  transfers between devices with their start and end apart: 13, of which 4 were waited for; matrix products, arithmetic and copies ran while one was open for 0% of the time, Pallas kernels for 74%

profile of v3, /device:TPU:106, one launch (start us, length us, event | category | flops | bytes accessed | tf_op | source)
XLA Modules:
  0.0 212.1 jit_solution(591419617904278633)
XLA Ops:
  0.6 0.0 copy-start.3
  0.6 0.0 copy-start.1
  0.7 0.0 copy-start.2
  0.7 0.0 copy-start
  0.7 0.0 copy-start.5
  0.7 0.0 copy-start.4
  0.7 1.0 pad_maximum_fusion.1.refs_0_.refs_4_
  1.7 0.1 collective-permute-start
  1.8 1.6 collective-permute-start.1
  3.4 0.5 collective-permute-start.2
  3.8 5.0 %collective-permute-done = bf16[384,256]{1,0:T(8,128)(2,1)S(1)} collective-permute-done((bf16[384,256]{1,0:T(8,128)(2,1)S(1)}, bf16[384,256]{1,0:T(8,128)(2,1)S(1)}, u32[]{:S(2)}, u32[]{:S(2)}) %collective-permute-start) | collective-permute-done | bytes 196640 | tf_op jit(solution)/shard_map/ppermute | solution.py:416
  8.8 11.8 %collective-permute-done.1 = bf16[384,256]{1,0:T(8,128)(2,1)S(1)} collective-permute-done((bf16[384,256]{1,0:T(8,128)(2,1)S(1)}, bf16[384,256]{1,0:T(8,128)(2,1)S(1)}, u32[]{:S(2)}, u32[]{:S(2)}) %collective-permute-start.1) | collective-permute-done | bytes 196640 | tf_op jit(solution)/shard_map/ppermute | solution.py:416
  20.6 0.0 collective-permute-done.2
  20.6 0.1 pad_maximum_fusion.refs_0_.refs_9_
  20.7 1.6 collective-permute-start.3
  22.3 0.5 collective-permute-start.4
  22.8 1.7 collective-permute-start.9
  24.5 0.3 collective-permute-start.7
  24.8 0.0 copy-done.3
  24.8 0.0 copy-done.1
  24.8 0.0 copy-done.2
  24.8 0.0 copy-done
  24.8 0.0 copy-done.5
  24.8 0.9 prepare.1
  25.7 5.5 %collective-permute-start.11 = (bf16[272,128]{1,0:T(8,128)(2,1)S(1)}, bf16[272,128]{1,0:T(8,128)(2,1)S(1)}, u32[]{:S(2)}, u32[]{:S(2)}) collective-permute-start(bf16[272,128]{1,0:T(8,128)(2,1)S(1)} %get-tuple-element.29), channel_id=1, source_target_pairs={{0,1},{1,0},{2,3},{3,2},{4,5},{5,4},{6,7},{7,6},{8,9},{9,8},{10,11... | collective-permute-start | bytes 208904 | tf_op jit(solution)/shard_map/ppermute | solution.py:420
  31.2 0.1 pad_add_fusion.place_ref.refs_0_
  31.3 2.8 %collective-permute-done.11.ask.refs_1_ = bf16[272,128]{1,0:T(8,128)(2,1)S(1)} collective-permute-done((bf16[272,128]{1,0:T(8,128)(2,1)S(1)}, bf16[272,128]{1,0:T(8,128)(2,1)S(1)}, u32[]{:S(2)}, u32[]{:S(2)}) %collective-permute-start.11) | collective-permute-done | bytes 69664 | tf_op jit(solution)/shard_map/ppermute | solution.py:420
  34.1 0.0 copy-done.4
  34.1 0.8 count.1
  35.0 5.4 %collective-permute-done.9.refs_2_.refs_6_ = bf16[384,256]{1,0:T(8,128)(2,1)S(1)} collective-permute-done((bf16[384,256]{1,0:T(8,128)(2,1)S(1)}, bf16[384,256]{1,0:T(8,128)(2,1)S(1)}, u32[]{:S(2)}, u32[]{:S(2)}) %collective-permute-start.9) | collective-permute-done | bytes 196640 | tf_op jit(solution)/shard_map/ppermute | solution.py:416
  40.4 0.6 collective-permute-start.10
  41.0 0.0 collective-permute-done.7.refs_1_.refs_5_
  41.0 1.6 collective-permute-start.8
  42.6 0.0 copy-start.6
  42.6 1.1 copy-done.6
  43.7 7.0 %shard_map.112 = (f32[8,384,128]{2,1,0:T(8,128)S(1)}, f32[8,384,128]{2,1,0:T(8,128)S(1)}, f32[8,384,128]{2,1,0:T(8,128)S(1)}) custom-call(s32[2]{0:T(128)S(1)} %pad_add_fusion.place_ref.refs_0_, bf16[384,1024]{1,0:T(8,128)(2,1)S(1)} %bitcast.19, bf16[384,256]{1,0:T(8,128)(2,1)S(1)} %pad_maximum_fusion.1.refs_0_.refs_4_, ...), custom_call_target="tpu_custom_call" | custom-call | flops 1811939328 | bytes 1048576 | tf_op jit(solution)/shard_map/pallas_call | solution.py:245
  50.7 0.0 collective-permute-done.3.refs_0_.refs_10_
  50.7 0.1 slice.16
  50.8 1.5 collective-permute-start.5
  52.3 0.0 collective-permute-done.4.refs_1_.refs_11_
  52.3 0.1 slice.17
  52.3 0.9 collective-permute-start.6
  53.2 5.1 %shard_map.113 = (f32[8,384,128]{2,1,0:T(8,128)S(1)}, f32[8,384,128]{2,1,0:T(8,128)S(1)}, f32[8,384,128]{2,1,0:T(8,128)S(1)}) custom-call(s32[2]{0:T(128)S(1)} %pad_add_fusion.place_ref.refs_0_, bf16[384,1024]{1,0:T(8,128)(2,1)S(1)} %bitcast.20, bf16[3,384,256]{2,1,0:T(8,128)(2,1)S(1)} %pad_maximum_fusion.refs_0_.refs_9_, ...), custom_call_target="tpu_custom_call", output_to_operand_aliasing={{0}: (3, {})} | custom-call | flops 2415919104 | bytes 1048576 | tf_op jit(solution)/shard_map/pallas_call | solution.py:245
  58.4 0.0 collective-permute-done.10.refs_3_.refs_8_
  58.4 0.0 collective-permute-done.8.refs_2_.refs_7_
  58.4 6.6 %shard_map.114 = (f32[8,384,128]{2,1,0:T(8,128)S(1)}, f32[8,384,128]{2,1,0:T(8,128)S(1)}, f32[8,384,128]{2,1,0:T(8,128)S(1)}) custom-call(s32[2]{0:T(128)S(1)} %pad_add_fusion.place_ref.refs_0_, bf16[384,1024]{1,0:T(8,128)(2,1)S(1)} %bitcast.21, bf16[3,384,256]{2,1,0:T(8,128)(2,1)S(1)} %collective-permute-done.3.refs_0_.refs_10_, ...), custom_call_target="tpu_custom_call", output_to_operand_aliasing={{0}: (6, {})} | custom-call | flops 2415919104 | bytes 1048576 | tf_op jit(solution)/shard_map/pallas_call | solution.py:245
  65.0 0.0 collective-permute-done.5.refs_2_.refs_12_
  65.0 0.0 collective-permute-done.6.refs_3_.refs_13_
  65.1 3.6 %context.1 = bf16[400,128]{1,0:T(8,128)(2,1)S(1)} custom-call(s32[2]{0:T(128)S(1)} %pad_add_fusion.place_ref.refs_0_, bf16[272,128]{1,0:T(8,128)(2,1)S(1)} %collective-permute-done.11.ask.refs_1_, f32[16,32,384]{2,1,0:T(8,128)S(1)} %get-tuple-element.30.refs_2_, bf16[16,64,384]{2,1,0:T(8,128)(2,1)S(1)} %get-tuple-element.31.refs_3_, ...), custom_call_target="tpu_custom_call" | custom-call | flops 805306368 | bytes 4194304 | tf_op jit(solution)/shard_map/context/pallas_call | solution.py:362
  68.7 5.5 %collective-permute-start.12 = (bf16[400,128]{1,0:T(8,128)(2,1)S(1)}, bf16[400,128]{1,0:T(8,128)(2,1)S(1)}, u32[]{:S(2)}, u32[]{:S(2)}) collective-permute-start(bf16[400,128]{1,0:T(8,128)(2,1)S(1)} %context.1), channel_id=1, source_target_pairs={{0,1},{1,0},{2,3},{3,2},{4,5},{5,4},{6,7},{7,6},{8,9},{9,8},{10,11... | collective-permute-start | bytes 307208 | tf_op jit(solution)/shard_map/ppermute | solution.py:420
  74.2 137.1 %shard_map.115 = bf16[384,1024]{1,0:T(8,128)(2,1)} custom-call(s32[2]{0:T(128)S(1)} %pad_add_fusion.place_ref.refs_0_, bf16[384,1024]{1,0:T(8,128)(2,1)S(1)} %bitcast.22, bf16[3,384,256]{2,1,0:T(8,128)(2,1)S(1)} %collective-permute-done.3.refs_0_.refs_10_, bf16[3,384,256]{2,1,0:T(8,128)(2,1)S(1)} %collective-permute-done.4.refs_1_.refs_11_, ...), custom_call_target="tpu_custom_call" | custom-call | flops 3019898880 | bytes 1048576 | tf_op jit(solution)/shard_map/pallas_call | solution.py:245
  211.2 0.0 collective-permute-done.12.back
  211.2 0.9 finish.1
  (2 shorter events, 0.0 us)
Async XLA Ops:
  0.6 24.2 %copy-start.3 = (s32[1,8,16]{2,1,0:T(8,128)S(1)}, s32[1,8,16]{2,1,0:T(8,128)}, u32[]{:S(2)}) copy-start(s32[1,8,16]{2,1,0:T(8,128)} %param.15) | copy-start | bytes 1540
  0.6 24.2 %copy-start.1 = (bf16[1,8,4,128]{3,2,1,0:T(4,128)(2,1)S(1)}, bf16[1,8,4,128]{3,2,1,0:T(4,128)(2,1)}, u32[]{:S(2)}) copy-start(bf16[1,8,4,128]{3,2,1,0:T(4,128)(2,1)} %param.13) | copy-start | bytes 24580
  0.7 24.2 %copy-start.2 = (bf16[1,8,4,128]{3,2,1,0:T(4,128)(2,1)S(1)}, bf16[1,8,4,128]{3,2,1,0:T(4,128)(2,1)}, u32[]{:S(2)}) copy-start(bf16[1,8,4,128]{3,2,1,0:T(4,128)(2,1)} %param.14) | copy-start | bytes 24580
  0.7 24.2 %copy-start = (bf16[1,8,4,1024]{3,2,1,0:T(4,128)(2,1)S(1)}, bf16[1,8,4,1024]{3,2,1,0:T(4,128)(2,1)}, u32[]{:S(2)}) copy-start(bf16[1,8,4,1024]{3,2,1,0:T(4,128)(2,1)} %param.12) | copy-start | bytes 196612
  0.7 24.2 %copy-start.5 = (s32[1,8]{1,0:T(1,128)S(1)}, s32[1,8]{1,0:T(1,128)}, u32[]{:S(2)}) copy-start(s32[1,8]{1,0:T(1,128)} %length.1) | copy-start | bytes 100
  0.7 33.5 %copy-start.4 = (bf16[8,128]{1,0:T(8,128)(2,1)S(1)}, bf16[8,128]{1,0:T(8,128)(2,1)}, u32[]{:S(2)}) copy-start(bf16[8,128]{1,0:T(8,128)(2,1)} %check.1) | copy-start | bytes 6148
  1.7 7.1 %collective-permute-start = (bf16[384,256]{1,0:T(8,128)(2,1)S(1)}, bf16[384,256]{1,0:T(8,128)(2,1)S(1)}, u32[]{:S(2)}, u32[]{:S(2)}) collective-permute-start(bf16[384,256]{1,0:T(8,128)(2,1)S(1)} %pad_maximum_fusion.1.refs_0_.refs_4_), channel_id=1, source_target_pairs={{0,64},{64,128},{128,192},{192,0},{1,65},{65,129},{129,193},{193,1... | collective-permute-start | bytes 589832 | tf_op jit(solution)/shard_map/ppermute | solution.py:416
  1.8 18.8 %collective-permute-start.1 = (bf16[384,256]{1,0:T(8,128)(2,1)S(1)}, bf16[384,256]{1,0:T(8,128)(2,1)S(1)}, u32[]{:S(2)}, u32[]{:S(2)}) collective-permute-start(bf16[384,256]{1,0:T(8,128)(2,1)S(1)} %pad_maximum_fusion.1.refs_0_.refs_4_), channel_id=1, source_target_pairs={{0,128},{64,192},{128,0},{192,64},{1,129},{65,193},{129,1},{193,65... | collective-permute-start | bytes 589832 | tf_op jit(solution)/shard_map/ppermute | solution.py:416
  3.4 17.3 %collective-permute-start.2 = (bf16[384,256]{1,0:T(8,128)(2,1)S(1)}, bf16[384,256]{1,0:T(8,128)(2,1)S(1)}, u32[]{:S(2)}, u32[]{:S(2)}) collective-permute-start(bf16[384,256]{1,0:T(8,128)(2,1)S(1)} %pad_maximum_fusion.1.refs_0_.refs_4_), channel_id=1, source_target_pairs={{0,192},{64,0},{128,64},{192,128},{1,193},{65,1},{129,65},{193,129... | collective-permute-start | bytes 589832 | tf_op jit(solution)/shard_map/ppermute | solution.py:416
  20.7 30.0 %collective-permute-start.3 = (bf16[3,384,256]{2,1,0:T(8,128)(2,1)S(1)}, bf16[3,384,256]{2,1,0:T(8,128)(2,1)S(1)}, u32[]{:S(2)}, u32[]{:S(2)}) collective-permute-start(bf16[3,384,256]{2,1,0:T(8,128)(2,1)S(1)} %pad_maximum_fusion.refs_0_.refs_9_), channel_id=1, source_target_pairs={{0,16},{16,32},{32,48},{48,0},{1,17},{17,33},{33,49},{49,1},{2,18}... | collective-permute-start | bytes 1769480 | tf_op jit(solution)/shard_map/ppermute | solution.py:416
  22.3 30.0 %collective-permute-start.4 = (bf16[3,384,256]{2,1,0:T(8,128)(2,1)S(1)}, bf16[3,384,256]{2,1,0:T(8,128)(2,1)S(1)}, u32[]{:S(2)}, u32[]{:S(2)}) collective-permute-start(bf16[3,384,256]{2,1,0:T(8,128)(2,1)S(1)} %pad_maximum_fusion.refs_0_.refs_9_), channel_id=1, source_target_pairs={{0,48},{16,0},{32,16},{48,32},{1,49},{17,1},{33,17},{49,33},{2,50}... | collective-permute-start | bytes 1769480 | tf_op jit(solution)/shard_map/ppermute | solution.py:416
  22.8 17.6 %collective-permute-start.9 = (bf16[384,256]{1,0:T(8,128)(2,1)S(1)}, bf16[384,256]{1,0:T(8,128)(2,1)S(1)}, u32[]{:S(2)}, u32[]{:S(2)}) collective-permute-start(bf16[384,256]{1,0:T(8,128)(2,1)S(1)} %pad_maximum_fusion.1.refs_0_.refs_4_), channel_id=1, source_target_pairs={{0,48},{16,0},{32,16},{48,32},{1,49},{17,1},{33,17},{49,33},{2,50}... | collective-permute-start | bytes 589832 | tf_op jit(solution)/shard_map/ppermute | solution.py:416
  24.5 16.5 %collective-permute-start.7 = (bf16[384,256]{1,0:T(8,128)(2,1)S(1)}, bf16[384,256]{1,0:T(8,128)(2,1)S(1)}, u32[]{:S(2)}, u32[]{:S(2)}) collective-permute-start(bf16[384,256]{1,0:T(8,128)(2,1)S(1)} %pad_maximum_fusion.1.refs_0_.refs_4_), channel_id=1, source_target_pairs={{0,16},{16,32},{32,48},{48,0},{1,17},{17,33},{33,49},{49,1},{2,18}... | collective-permute-start | bytes 589832 | tf_op jit(solution)/shard_map/ppermute | solution.py:416
  25.7 8.4 %collective-permute-start.11 = (bf16[272,128]{1,0:T(8,128)(2,1)S(1)}, bf16[272,128]{1,0:T(8,128)(2,1)S(1)}, u32[]{:S(2)}, u32[]{:S(2)}) collective-permute-start(bf16[272,128]{1,0:T(8,128)(2,1)S(1)} %get-tuple-element.29), channel_id=1, source_target_pairs={{0,1},{1,0},{2,3},{3,2},{4,5},{5,4},{6,7},{7,6},{8,9},{9,8},{10,11... | collective-permute-start | bytes 208904 | tf_op jit(solution)/shard_map/ppermute | solution.py:420
  40.4 18.0 %collective-permute-start.10 = (bf16[384,128]{1,0:T(8,128)(2,1)S(1)}, bf16[384,128]{1,0:T(8,128)(2,1)S(1)}, u32[]{:S(2)}, u32[]{:S(2)}) collective-permute-start(bf16[384,128]{1,0:T(8,128)(2,1)S(1)} %slice.19), channel_id=1, source_target_pairs={{0,48},{16,0},{32,16},{48,32},{1,49},{17,1},{33,17},{49,33},{2,50}... | collective-permute-start | bytes 294920 | tf_op jit(solution)/shard_map/ppermute | solution.py:416
  41.0 17.3 %collective-permute-start.8 = (bf16[384,128]{1,0:T(8,128)(2,1)S(1)}, bf16[384,128]{1,0:T(8,128)(2,1)S(1)}, u32[]{:S(2)}, u32[]{:S(2)}) collective-permute-start(bf16[384,128]{1,0:T(8,128)(2,1)S(1)} %slice.18), channel_id=1, source_target_pairs={{0,16},{16,32},{32,48},{48,0},{1,17},{17,33},{33,49},{49,1},{2,18}... | collective-permute-start | bytes 294920 | tf_op jit(solution)/shard_map/ppermute | solution.py:416
  42.6 1.1 copy-start.6
  50.8 14.2 %collective-permute-start.5 = (bf16[3,384,128]{2,1,0:T(8,128)(2,1)S(1)}, bf16[3,384,128]{2,1,0:T(8,128)(2,1)S(1)}, u32[]{:S(2)}, u32[]{:S(2)}) collective-permute-start(bf16[3,384,128]{2,1,0:T(8,128)(2,1)S(1)} %slice.16), channel_id=1, source_target_pairs={{0,16},{16,32},{32,48},{48,0},{1,17},{17,33},{33,49},{49,1},{2,18}... | collective-permute-start | bytes 884744 | tf_op jit(solution)/shard_map/ppermute | solution.py:416
  52.3 12.7 %collective-permute-start.6 = (bf16[3,384,128]{2,1,0:T(8,128)(2,1)S(1)}, bf16[3,384,128]{2,1,0:T(8,128)(2,1)S(1)}, u32[]{:S(2)}, u32[]{:S(2)}) collective-permute-start(bf16[3,384,128]{2,1,0:T(8,128)(2,1)S(1)} %slice.17), channel_id=1, source_target_pairs={{0,48},{16,0},{32,16},{48,32},{1,49},{17,1},{33,17},{49,33},{2,50}... | collective-permute-start | bytes 884744 | tf_op jit(solution)/shard_map/ppermute | solution.py:416
  68.7 142.5 %collective-permute-start.12 = (bf16[400,128]{1,0:T(8,128)(2,1)S(1)}, bf16[400,128]{1,0:T(8,128)(2,1)S(1)}, u32[]{:S(2)}, u32[]{:S(2)}) collective-permute-start(bf16[400,128]{1,0:T(8,128)(2,1)S(1)} %context.1), channel_id=1, source_target_pairs={{0,1},{1,0},{2,3},{3,2},{4,5},{5,4},{6,7},{7,6},{8,9},{9,8},{10,11... | collective-permute-start | bytes 307208 | tf_op jit(solution)/shard_map/ppermute | solution.py:420
